TPU v7x, 32 devices: a whole 2x2x4 slice. The times are simulated.
32 devices in a mesh: sp: 4 (over x, core), tp: 8 (over z, y).
Axes of the slice: x: 2, y: 2, z: 4, core: 2. Of those that a mesh axis runs over, the one named last changes fastest.
Arguments:
- tokens: bfloat16 [8, 220, 4096], P(None, 'sp'), may hold values from -6 to 6
- modulation: float32 [6, 4096], replicated, may hold values from -2.5 to 2.5
- w_qkv: bfloat16 [4096, 3, 4096], P('sp', None, 'tp'), may hold values from -4 to 4
- w_out: bfloat16 [4096, 4096], P('tp', 'sp'), may hold values from -0.09375 to 0.09375
- w_up: bfloat16 [4096, 16384], P('sp', 'tp'), may hold values from -0.09375 to 0.09375
- w_down: bfloat16 [16384, 4096], P('tp', 'sp'), may hold values from -0.046875 to 0.046875
Outputs:
- block_out: bfloat16 [8, 220, 4096], P(None, 'sp', 'tp')
All inputs are finite; a program needn't handle non-finite values.
Results may differ from a plain program's by a relative error of at most 0.012.
Values may be sent and summed in bfloat16 or wider, within the bound.
A program may use at most 128 MiB of HBM per device.

v0:
```python
import jax
import jax.numpy as jnp
from jax import lax
from jax.sharding import PartitionSpec as P

DH = 128


EPSILON = 1e-06


def normalize(tok_rows, shift_vec, scale_vec):
    values = tok_rows.astype(jnp.float32)
    center = jnp.mean(values, axis=-1, keepdims=True)
    spread = jnp.mean(jnp.square(values - center), axis=-1, keepdims=True)
    scaled = (values - center) * lax.rsqrt(spread + EPSILON)
    return (scaled * (1.0 + scale_vec) + shift_vec).astype(jnp.bfloat16)


def project_rows(operand, weight, einsum_form):
    return jnp.einsum(
        einsum_form,
        operand,
        lax.all_gather(weight, "sp", axis=0, tiled=True),
        preferred_element_type=jnp.float32,
    )


def project_cols(operand, weight, einsum_form, leading):
    portion = lax.all_gather(weight, "sp", axis=1, tiled=True)
    shaped = portion.reshape(leading + (portion.shape[1],))
    return jnp.einsum(einsum_form, operand, shaped, preferred_element_type=jnp.float32)


def attend_items(pieces):
    queries, key_rows, values = pieces
    factor = queries.shape[-1] ** (-0.5)

    def single(triple):
        query_one, key_one, value_one = triple
        scores = (
            lax.dot_general(
                query_one, key_one, (((1,), (1,)), ((), ())), preferred_element_type=jnp.float32
            )
            * factor
        )
        row_max = jnp.max(scores, axis=1, keepdims=True)
        raw_weights = jnp.exp(scores - row_max)
        att_weights = (raw_weights / jnp.sum(raw_weights, axis=1, keepdims=True)).astype(
            jnp.bfloat16
        )
        return jnp.dot(att_weights, value_one, preferred_element_type=jnp.float32).astype(
            jnp.bfloat16
        )

    result = lax.map(single, (queries[0], key_rows[0], values[0]))
    return result[None]


def attention_combine(base, partial_value, gate):
    summed = lax.psum(partial_value.astype(jnp.bfloat16), "tp").astype(jnp.float32)
    full = (base.astype(jnp.float32) + gate * summed).astype(jnp.bfloat16)
    return full


def mlp_combine(base, partial_value, gate):
    tp_count = lax.axis_size("tp")
    width = base.shape[2] // tp_count
    offset = lax.axis_index("tp") * width
    base_mine = lax.dynamic_slice_in_dim(base, offset, width, 2).astype(jnp.float32)
    gate_mine = lax.dynamic_slice_in_dim(gate, offset, width, 0)
    share = lax.psum_scatter(
        partial_value.astype(jnp.bfloat16), "tp", scatter_dimension=2, tiled=True
    ).astype(jnp.float32)
    return (base_mine + gate_mine * share).astype(jnp.bfloat16)


def shards(tokens, modulation, w_qkv, w_out, w_up, w_down):
    frames, patches, width = tokens.shape
    heads_local = w_qkv.shape[2] // DH
    sp_count = lax.axis_size("sp")
    items_dev = heads_local * frames // sp_count
    mod_a = normalize(tokens, modulation[0], modulation[1])
    weight_qkv = w_qkv.reshape(w_qkv.shape[0], 3, heads_local, DH)
    projected = project_rows(mod_a, weight_qkv, "fpd,dshe->shfpe").astype(jnp.bfloat16)
    projected = projected.reshape(3, sp_count, items_dev, patches, DH)
    attended = attend_items(
        (
            lax.all_to_all(projected[0], "sp", split_axis=0, concat_axis=2, tiled=True),
            lax.all_to_all(projected[1], "sp", split_axis=0, concat_axis=2, tiled=True),
            lax.all_to_all(projected[2], "sp", split_axis=0, concat_axis=2, tiled=True),
        )
    )
    returned = lax.all_to_all(attended, "sp", split_axis=2, concat_axis=0, tiled=True)
    returned = returned.reshape(heads_local, frames, patches, DH)
    partial_attn = project_cols(returned, w_out, "hfpd,hde->fpe", (heads_local, DH))
    middle = attention_combine(tokens, partial_attn, modulation[2])
    mod_b = normalize(middle, modulation[3], modulation[4])
    up_proj = project_rows(mod_b, w_up, "fpd,dc->fpc")
    hidden = jax.nn.gelu(up_proj, approximate=True).astype(jnp.bfloat16)
    partial_mlp = project_cols(hidden, w_down, "fpk,kc->fpc", (w_down.shape[0],))
    return mlp_combine(middle, partial_mlp, modulation[5])


def solution(mesh):
    placed = (
        P(None, "sp", None),
        P(),
        P("sp", None, "tp"),
        P("tp", "sp"),
        P("sp", "tp"),
        P("tp", "sp"),
    )
    return jax.shard_map(
        shards, mesh=mesh, in_specs=placed, out_specs=P(None, "sp", "tp"), check_vma=False
    )
```

profile of v0, /device:TPU:0, one launch (start us, length us, event | category | flops | bytes accessed | tf_op | source)
XLA Modules:
  0.0 655.9 jit_solution(7131236097919553995)
XLA Ops:
  6.5 3.2 copy.22
  9.7 2.8 copy.23
  12.6 0.0 all-gather.7.cloned.1.call-start
  12.6 0.7 all-gather.7.cloned.1.call-update
  13.3 0.1 fusion.82
  13.4 5.8 convert_reduce_fusion
  19.2 3.9 fusion.23
  23.1 74.4 %all-gather.5.cloned.1.call-done = bf16[4096,3,4,128]{3,0,2,1:T(8,128)(2,1)} async-done(((bf16[1024,3,4,128]{3,0,2,1:T(8,128)(2,1)}), bf16[4096,3,4,128]{3,0,2,1:T(8,128)(2,1)}) %all-gather.5.cloned.1.call-update) | async-done | bytes 12582928 | tf_op jit(solution)/shard_map/all_gather | solution.py:24
  97.5 18.3 %fusion.69 = bf16[3,4,8,55,128]{4,3,1,0,2:T(8,128)(2,1)S(1)} fusion(bf16[4096,3,4,128]{3,0,2,1:T(8,128)(2,1)} %all-gather.5.cloned.1.call-done, f32[4096]{0:T(1024)S(1)} %bitcast.107, f32[4096]{0:T(1024)S(1)} %bitcast.108, f32[8,55]{1,0:T(8,128)S(1)} %add_rsqrt_fusion.1, f32[8,55]{1,0:T(8,128)S(1)} %broadcast_multiply_fusion.1, bf16[8,55,4096]{2,0,1:T(8,128)(2,1)} %param.8), kind=kOutput, calls=%fused_computation.64 | convolution fusion | flops 5547970560 | bytes 17575360 | tf_op jit(solution)/shard_map/fpd,dshe->shfpe/dot_general | solution.py:21
  115.8 0.1 slice_bitcast_fusion
  115.9 0.9 copy.24
  116.9 3.5 all-to-all-start
  120.3 0.9 copy.25
  121.3 12.3 %all-to-all-done = bf16[4,8,55,128]{3,1,2,0:T(8,128)(2,1)S(1)} async-done(((bf16[4,8,55,128]{3,1,2,0:T(8,128)(2,1)}), bf16[4,8,55,128]{3,1,2,0:T(8,128)(2,1)S(1)}, u32[]{:S(2)}, u32[]{:S(2)}) %all-to-all-start) | async-done | bytes 450592 | tf_op jit(solution)/shard_map/all_to_all | solution.py:89
  133.6 3.5 all-to-all-start.1
  137.1 0.9 copy.26
  138.0 7.0 %all-to-all-done.1 = bf16[4,8,55,128]{3,1,2,0:T(8,128)(2,1)S(1)} async-done(((bf16[4,8,55,128]{3,1,2,0:T(8,128)(2,1)}), bf16[4,8,55,128]{3,1,2,0:T(8,128)(2,1)S(1)}, u32[]{:S(2)}, u32[]{:S(2)}) %all-to-all-start.1) | async-done | bytes 450592 | tf_op jit(solution)/shard_map/all_to_all | solution.py:90
  145.0 3.5 all-to-all-start.2
  148.5 0.1 copy.27
  148.6 0.1 copy.28
  148.7 7.8 %all-to-all-done.2 = bf16[4,8,55,128]{3,1,2,0:T(8,128)(2,1)S(1)} async-done(((bf16[4,8,55,128]{3,1,2,0:T(8,128)(2,1)}), bf16[4,8,55,128]{3,1,2,0:T(8,128)(2,1)S(1)}, u32[]{:S(2)}, u32[]{:S(2)}) %all-to-all-start.2) | async-done | bytes 450592 | tf_op jit(solution)/shard_map/all_to_all | solution.py:91
  156.5 0.1 copy.29
  156.6 4.6 while.10
  156.6 0.2 fusion.89
  156.8 0.1 fusion.90
  156.9 0.2 fusion.91
  157.2 0.2 fusion.89
  157.4 0.1 fusion.90
  157.5 0.2 fusion.91
  157.7 0.2 fusion.89
  158.0 0.1 fusion.90
  158.0 0.2 fusion.91
  158.3 0.2 fusion.89
  158.5 0.1 fusion.90
  158.6 0.2 fusion.91
  158.9 0.2 fusion.89
  159.1 0.1 fusion.90
  159.2 0.2 fusion.91
  159.4 0.2 fusion.89
  159.7 0.1 fusion.90
  159.8 0.2 fusion.91
  160.0 0.2 fusion.89
  160.3 0.1 fusion.90
  160.3 0.2 fusion.91
  160.6 0.2 fusion.89
  160.8 0.1 fusion.90
  160.9 0.2 fusion.91
  161.2 0.9 copy.52
  162.1 3.5 all-to-all-start.3
  165.6 7.9 %all-to-all-done.3 = bf16[1,8,220,128]{3,1,0,2:T(8,128)(2,1)S(1)} async-done(((bf16[1,8,220,128]{3,1,0,2:T(8,128)(2,1)}), bf16[1,8,220,128]{3,1,0,2:T(8,128)(2,1)S(1)}, u32[]{:S(2)}, u32[]{:S(2)}) %all-to-all-start.3) | async-done | bytes 450592 | tf_op jit(solution)/shard_map/all_to_all | solution.py:94
  173.6 5.7 bitcast_convert_fusion
  179.4 0.5 all-gather.11.cloned.1.call-update
  180.0 0.5 all-gather.9.cloned.1.call-update
  180.5 0.3 reduce-scatter.2.cloned.1.call-start
  180.8 141.6 %all-reduce.2.cloned.1.call-done = bf16[8,55,4096]{2,1,0:T(8,128)(2,1)} async-done(((bf16[8,55,4096]{2,1,0:T(8,128)(2,1)}), bf16[8,55,4096]{2,1,0:T(8,128)(2,1)}) %all-reduce.2.cloned.1.call-update) | async-done | bytes 3604496 | tf_op jit(solution)/shard_map/psum | solution.py:61
  322.4 8.3 %convert_reduce_fusion.1 = (f32[8,55]{1,0:T(8,128)S(1)}, bf16[8,55,4096]{2,1,0:T(8,128)(2,1)S(1)}) fusion(bf16[8,55,4096]{2,1,0:T(8,128)(2,1)} %all-reduce.2.cloned.1.call-done, f32[4096]{0:T(1024)S(1)} %bitcast.104, bf16[8,55,4096]{2,0,1:T(8,128)(2,1)} %param.8), kind=kLoop, calls=%fused_computation.27 | loop fusion | flops 12615240 | bytes 10831584 | tf_op jit(solution)/shard_map/reduce_sum | solution.py:14
  330.7 2.0 copy-done.1
  332.7 1.1 fusion.27
  333.8 94.7 %all-gather.11.cloned.1.call-done = bf16[2048,4096]{1,0:T(8,128)(2,1)} async-done(((bf16[2048,1024]{1,0:T(8,128)(2,1)}), bf16[2048,4096]{1,0:T(8,128)(2,1)}) %all-gather.11.cloned.1.call-update) | async-done | bytes 16777232 | tf_op jit(solution)/shard_map/all_gather | solution.py:30
  428.5 107.3 %all-gather.9.cloned.1.call-done = bf16[4096,2048]{1,0:T(8,128)(2,1)} async-done(((bf16[1024,2048]{1,0:T(8,128)(2,1)}), bf16[4096,2048]{1,0:T(8,128)(2,1)}) %all-gather.9.cloned.1.call-update) | async-done | bytes 16777232 | tf_op jit(solution)/shard_map/all_gather | solution.py:24
  535.9 29.4 %fusion.32 = bf16[8,55,4096]{2,1,0:T(8,128)(2,1)} fusion(bf16[2048,4096]{1,0:T(8,128)(2,1)} %all-gather.11.cloned.1.call-done, bf16[4096,2048]{1,0:T(8,128)(2,1)} %all-gather.9.cloned.1.call-done, bf16[8,55,4096]{2,1,0:T(8,128)(2,1)} %copy-done.1, f32[4096]{0:T(1024)S(1)} %bitcast.105, f32[4096]{0:T(1024)S(1)} %bitcast.106, f32[8,55]{1,0:T(8,128)S(1)} %add_rsqrt_fusion, ...), kind=kOutput, calls=%fused_computation.42 | convolution fusion | flops 14784675840 | bytes 40799680 | tf_op jit(solution)/shard_map/fpk,kc->fpc/dot_general | solution.py:32
  565.4 81.5 %reduce-scatter.2.cloned.1.call-done = bf16[8,55,512]{2,1,0:T(8,128)(2,1)} async-done(((bf16[8,55,4096]{2,1,0:T(8,128)(2,1)}), bf16[8,55,512]{2,1,0:T(8,128)(2,1)}) %reduce-scatter.2.cloned.1.call-update) | async-done | bytes 450576 | tf_op jit(solution)/shard_map/reduce_scatter | solution.py:72
  646.9 1.3 add_convert_fusion
  648.2 0.9 copy.32
  (19 shorter events, 0.2 us)
Async XLA Ops:
  6.5 91.0 %all-gather.5.cloned.1.call-start = ((), (), s32[]{:S(2)}) async-start(), calls=%async_computation.5 | async-start | bytes 15728640 | tf_op jit(solution)/shard_map/all_gather | solution.py:24
  9.7 3.6 copy-start.2
  12.6 153.1 %all-gather.7.cloned.1.call-start = ((), (), s32[]{:S(2)}) async-start(), calls=%async_computation.6 | async-start | bytes 5242880 | tf_op jit(solution)/shard_map/all_gather | solution.py:30
  13.3 5.9 copy-start
  116.9 16.7 %all-to-all-start = ((bf16[4,8,55,128]{3,1,2,0:T(8,128)(2,1)}), bf16[4,8,55,128]{3,1,2,0:T(8,128)(2,1)S(1)}, u32[]{:S(2)}, u32[]{:S(2)}) async-start(bf16[4,8,55,128]{3,1,2,0:T(8,128)(2,1)} %copy.24), calls=%async_computation | async-start | bytes 901120 | tf_op jit(solution)/shard_map/all_to_all | solution.py:89
  133.6 11.5 %all-to-all-start.1 = ((bf16[4,8,55,128]{3,1,2,0:T(8,128)(2,1)}), bf16[4,8,55,128]{3,1,2,0:T(8,128)(2,1)S(1)}, u32[]{:S(2)}, u32[]{:S(2)}) async-start(bf16[4,8,55,128]{3,1,2,0:T(8,128)(2,1)} %copy.25), calls=%async_computation.1 | async-start | bytes 901120 | tf_op jit(solution)/shard_map/all_to_all | solution.py:90
  145.0 11.5 %all-to-all-start.2 = ((bf16[4,8,55,128]{3,1,2,0:T(8,128)(2,1)}), bf16[4,8,55,128]{3,1,2,0:T(8,128)(2,1)S(1)}, u32[]{:S(2)}, u32[]{:S(2)}) async-start(bf16[4,8,55,128]{3,1,2,0:T(8,128)(2,1)} %copy.26), calls=%async_computation.2 | async-start | bytes 901120 | tf_op jit(solution)/shard_map/all_to_all | solution.py:91
  162.1 11.5 %all-to-all-start.3 = ((bf16[1,8,220,128]{3,1,0,2:T(8,128)(2,1)}), bf16[1,8,220,128]{3,1,0,2:T(8,128)(2,1)S(1)}, u32[]{:S(2)}, u32[]{:S(2)}) async-start(bf16[1,8,220,128]{3,1,0,2:T(8,128)(2,1)} %bitcast.90), calls=%async_computation.3 | async-start | bytes 901120 | tf_op jit(solution)/shard_map/all_to_all | solution.py:94
  165.6 156.8 %all-reduce.2.cloned.1.call-start = ((), (), s32[]{:S(2)}) async-start(), calls=%async_computation.7 | async-start | bytes 7340032 | tf_op jit(solution)/shard_map/psum | solution.py:61
  179.3 249.2 %all-gather.11.cloned.1.call-start = ((), (), s32[]{:S(2)}) async-start(), calls=%async_computation.9 | async-start | bytes 20971520 | tf_op jit(solution)/shard_map/all_gather | solution.py:30
  179.9 356.0 %all-gather.9.cloned.1.call-start = ((), (), s32[]{:S(2)}) async-start(), calls=%async_computation.8 | async-start | bytes 20971520 | tf_op jit(solution)/shard_map/all_gather | solution.py:24
  180.5 466.4 %reduce-scatter.2.cloned.1.call-start = ((), (), s32[]{:S(2)}) async-start(), calls=%async_computation.10 | async-start | bytes 4128768 | tf_op jit(solution)/shard_map/reduce_scatter | solution.py:72
  330.7 2.0 copy-start.1
Sparse Core Ops, SparseCore 0:
  12.7 84.7 all-gather.4
  99.1 39.4 all-gather.6
  179.4 142.8 all-reduce.1
  323.8 104.7 all-gather.10
  429.9 105.8 all-gather.8
  565.5 81.3 reduce-scatter.1
where the time goes:
time: 656 us
  waiting for transfers between devices  536 us (82%)
  matrix products  57.3 us (9%)
  other arithmetic  21.1 us (3%)
  starting transfers between devices  14.3 us (2%)
  between operations  13.6 us (2%)
  local copies, waits for them, and re-layouts  13 us (2%)
    all_gather x2, waiting for transfers between devices, project_rows(): lax.all_gather(weight, 'sp', axis=0, tiled=True)  182 us
    psum x1, waiting for transfers between devices, attention_combine(): lax.psum(partial_value.astype(jnp.bfloat16), 'tp').astype(jnp.float32)  142 us
    all_gather x2, waiting for transfers between devices, project_cols(): portion = lax.all_gather(weight, 'sp', axis=1, tiled=True)  94.7 us
    reduce_scatter x1, waiting for transfers between devices, mlp_combine(): lax.psum_scatter(partial_value.astype(jnp.bfloat16), 'tp', scatter_dimens...  81.5 us
    dot_general x2, matrix products, project_cols(): jnp.einsum(einsum_form, operand, shaped, preferred_element_type=jnp.float32)  35.2 us
    dot_general x1, matrix products, project_rows(): jnp.einsum(einsum_form, operand, lax.all_gather(weight, 'sp', axis=0, til...  18.3 us
    reduce_sum x2, other arithmetic, normalize(): center = jnp.mean(values, axis=-1, keepdims=True)  14.1 us
  transfers between devices with their start and end apart: 10, of which 9 were waited for; matrix products, arithmetic and copies ran while one was open for 7% of the time, Pallas kernels for 0%

commit v1 on v0

v1 whole, which is shorter than its diff:
```python
import math

import jax
import jax.numpy as jnp
from jax import lax
from jax.sharding import PartitionSpec as P

DH = 128
EPSILON = 1e-06
MLP_CHUNKS = 4
BF = jnp.bfloat16
F32 = jnp.float32


def normalize(tok_rows, shift_vec, scale_vec):
    values = tok_rows.astype(F32)
    center = jnp.mean(values, axis=-1, keepdims=True)
    spread = jnp.mean(jnp.square(values - center), axis=-1, keepdims=True)
    scaled = (values - center) * lax.rsqrt(spread + EPSILON)
    return (scaled * (1.0 + scale_vec) + shift_vec).astype(BF)


def reduce_scatter_sp(parts):
    sp_count, n, c = parts.shape
    chips = sp_count // 2
    me = lax.axis_index("sp")
    core, chip = me % 2, me // 2
    pairs = parts.reshape(chips, 2, n, c)
    away = lax.dynamic_index_in_dim(pairs, 1 - core, 1, keepdims=False)
    got = lax.ppermute(away, "sp", [(i, i ^ 1) for i in range(sp_count)])
    mine = lax.dynamic_index_in_dim(pairs, core, 1, keepdims=False)
    both = (mine.astype(F32) + got.astype(F32)).astype(BF)
    total = lax.dynamic_index_in_dim(both, chip, 0, keepdims=False).astype(F32)
    for k in range(1, chips):
        piece = lax.dynamic_index_in_dim(both, (chip + k) % chips, 0, keepdims=False)
        perm = [(i, ((i // 2 + k) % chips) * 2 + i % 2) for i in range(sp_count)]
        total = total + lax.ppermute(piece, "sp", perm).astype(F32)
    return total


def all_gather_sp(piece):
    n, c = piece.shape
    sp_count = lax.axis_size("sp")
    chips = sp_count // 2
    me = lax.axis_index("sp")
    core, chip = me % 2, me // 2
    out = jnp.zeros((chips, 2, n, c), piece.dtype)
    for k in range(chips):
        got = piece
        if k:
            perm = [(i, ((i // 2 + k) % chips) * 2 + i % 2) for i in range(sp_count)]
            got = lax.ppermute(piece, "sp", perm)
        other = lax.ppermute(got, "sp", [(i, i ^ 1) for i in range(sp_count)])
        at = (chip - k) % chips
        out = lax.dynamic_update_slice(out, got[None, None], (at, core, 0, 0))
        out = lax.dynamic_update_slice(out, other[None, None], (at, 1 - core, 0, 0))
    return out.reshape(sp_count, n, c)


def attend(queries, key_rows, values, key_ok):
    factor = queries.shape[-1] ** (-0.5)
    scores = jnp.einsum("iqe,ike->iqk", queries, key_rows, preferred_element_type=F32) * factor
    scores = jnp.where(key_ok, scores, -jnp.inf)
    raw = jnp.exp(scores - jnp.max(scores, axis=-1, keepdims=True))
    att_weights = (raw / jnp.sum(raw, axis=-1, keepdims=True)).astype(BF)
    return jnp.einsum("iqk,ike->iqe", att_weights, values, preferred_element_type=F32).astype(BF)


def shards(tokens, modulation, w_qkv, w_out, w_up, w_down):
    frames, patches, width = tokens.shape
    sp_count, tp_count = lax.axis_size("sp"), lax.axis_size("tp")
    sp_me, tp_me = lax.axis_index("sp"), lax.axis_index("tp")
    heads = w_qkv.shape[2] // DH
    slab = width // sp_count
    groups = math.gcd(frames, tp_count)
    sub, f_own = tp_count // groups, frames // groups
    unit = 8 * sub
    padded = -(-patches // unit) * unit
    part = padded // sub
    rows = sub * sp_count * part
    own_rows = f_own * sp_count * part

    padded_tokens = jnp.pad(tokens, ((0, 0), (0, padded - patches), (0, 0)))
    mine = lax.dynamic_slice(
        padded_tokens, ((tp_me // sub) * f_own, (tp_me % sub) * part, 0), (f_own, part, width)
    )
    mod_mine = normalize(mine, modulation[0], modulation[1])
    both = jnp.stack([mod_mine, mine]).reshape(2, f_own, part, sp_count, slab)
    both = lax.all_to_all(both, "sp", split_axis=3, concat_axis=2, tiled=False)
    mod_slab = both[0].reshape(own_rows, slab)
    tok_slab = both[1].reshape(own_rows, slab)
    mod_a = spread_rows(mod_slab, frames, sub, f_own, rows)

    at = jnp.arange(rows)
    key_ok = ((at // (sp_count * part)) * part + at % part) < patches

    chunks = 2 if frames % (2 * sp_count) == 0 else 1
    f_chunk = frames // chunks
    f_split = math.gcd(f_chunk, sp_count)
    h_split = sp_count // f_split
    f_mine, h_mine = f_chunk // f_split, heads // h_split
    w_flat = w_qkv.reshape(slab, 3 * heads * DH)
    attn_parts = []
    for c in range(chunks):
        lhs = mod_a[c * f_chunk : (c + 1) * f_chunk].reshape(f_chunk * rows, slab)
        proj = jnp.dot(lhs, w_flat, preferred_element_type=F32).astype(BF)
        if h_split > 1:
            proj = proj.reshape(f_split, f_mine * rows, 3, h_split, h_mine * DH)
            proj = jnp.transpose(proj, (0, 3, 1, 2, 4))
        proj = proj.reshape(sp_count, f_mine * rows, 3 * h_mine * DH)
        proj = reduce_scatter_sp(proj).astype(BF).reshape(f_mine, rows, 3, h_mine, DH)
        proj = jnp.transpose(proj, (2, 0, 3, 1, 4)).reshape(3, f_mine * h_mine, rows, DH)
        att = attend(proj[0], proj[1], proj[2], key_ok)
        att = jnp.transpose(att.reshape(f_mine, h_mine, rows, DH), (0, 2, 1, 3))
        att = all_gather_sp(att.reshape(f_mine * rows, h_mine * DH))
        if h_split > 1:
            att = att.reshape(f_split, h_split, f_mine * rows, h_mine * DH)
            att = jnp.transpose(att, (0, 2, 1, 3))
        att = att.reshape(f_chunk * rows, heads * DH)
        attn_parts.append(jnp.dot(att, w_out, preferred_element_type=F32).astype(BF))
    attn_part = jnp.concatenate(attn_parts, 0).reshape(tp_count, own_rows, slab)
    attn_sum = lax.psum_scatter(attn_part, "tp", scatter_dimension=0, tiled=False).astype(F32)

    mod_slice = lax.dynamic_slice_in_dim(modulation, sp_me * slab, slab, 1)
    middle = (tok_slab.astype(F32) + mod_slice[2] * attn_sum).astype(BF)

    values = middle.astype(F32)
    mean_s = jnp.mean(values, axis=-1)
    dev_s = jnp.sum(jnp.square(values - mean_s[:, None]), axis=-1)
    stats = lax.all_gather(jnp.stack([mean_s, dev_s]), "sp", axis=0)
    center = jnp.mean(stats[:, 0], axis=0)
    spread = (jnp.sum(stats[:, 1], 0) + slab * jnp.sum(jnp.square(stats[:, 0] - center), 0)) / width
    scaled = (values - center[:, None]) * lax.rsqrt(spread + EPSILON)[:, None]
    mod_b = (scaled * (1.0 + mod_slice[4]) + mod_slice[3]).astype(BF)
    mod_b = spread_rows(mod_b, frames, sub, f_own, rows).reshape(frames * rows, slab)

    hid = w_up.shape[1] // MLP_CHUNKS
    share = frames * rows // sp_count
    acc = None
    for c in range(MLP_CHUNKS):
        up = jnp.dot(mod_b, w_up[:, c * hid : (c + 1) * hid], preferred_element_type=F32)
        up = reduce_scatter_sp(up.astype(BF).reshape(sp_count, share, hid))
        hidden = jax.nn.gelu(up, approximate=True).astype(BF)
        hidden = all_gather_sp(hidden).reshape(frames * rows, hid)
        term = jnp.dot(hidden, w_down[c * hid : (c + 1) * hid], preferred_element_type=F32)
        acc = term if acc is None else acc + term
    mlp_part = acc.astype(BF).reshape(tp_count, own_rows, slab)
    mlp_sum = lax.psum_scatter(mlp_part, "tp", scatter_dimension=0, tiled=False).astype(F32)
    block = (middle.astype(F32) + mod_slice[5] * mlp_sum).astype(BF)

    block = block.reshape(f_own, sp_count, part, slab)
    block = lax.all_to_all(block, "sp", split_axis=1, concat_axis=2, tiled=False)
    block = block.reshape(f_own, part, width)
    block = block.reshape(f_own, part, tp_count, width // tp_count)
    block = lax.all_to_all(block, "tp", split_axis=2, concat_axis=0, tiled=False)
    block = block.reshape(groups, sub, f_own, part, width // tp_count)
    block = jnp.transpose(block, (0, 2, 1, 3, 4)).reshape(frames, padded, width // tp_count)
    return block[:, :patches]


def spread_rows(own, frames, sub, f_own, rows):
    whole = lax.all_gather(own, "tp", axis=0, tiled=True)
    return whole.reshape(frames, rows, own.shape[1])


def solution(mesh):
    placed = (
        P(None, "sp", None),
        P(),
        P("sp", None, "tp"),
        P("tp", "sp"),
        P("sp", "tp"),
        P("tp", "sp"),
    )
    return jax.shard_map(
        shards, mesh=mesh, in_specs=placed, out_specs=P(None, "sp", "tp"), check_vma=False
    )
```

time: 656 us -> 563 us (0.86)
  waiting for transfers between devices: 536 us -> 374 us
  blocking collectives: 0 us -> 50.2 us
  local copies, waits for them, and re-layouts: 13 us -> 33.8 us
  matrix products: 57.3 us -> 44.7 us
    all_gather x4 -> x2, waiting for transfers between devices: 276 us -> 128 us  [spread_rows(): whole = lax.all_gather(own, 'tp', axis=0, tiled=True)]
    psum x1 -> x0, waiting for transfers between devices: 142 us -> none  [attention_combine(): lax.psum(partial_value.astype(jnp.bfloat16), 'tp').astype(jnp.float32)]
    ppermute x0 -> x30, waiting for transfers between devices: none -> 88.7 us  [the longest x6 46.6 us: reduce_scatter_sp(): total = total + lax.ppermute(piece, 'sp', perm).astype(F32)]
    reduce_scatter x1 -> x2, waiting for transfers between devices: 81.5 us -> 158 us  [the longest x1 79.9 us: shards(): lax.psum_scatter(mlp_part, 'tp', scatter_dimension=0, tiled=False)]
    all_to_all x0 -> x3, blocking collectives: none -> 45 us  [the longest x1 17.3 us: shards(): lax.all_to_all(block, 'tp', split_axis=2, concat_axis=0, tiled=False)]
    all_to_all x4 -> x0, waiting for transfers between devices: 35.1 us -> none  [the longest x1 12.3 us: shards(): lax.all_to_all(projected[0], 'sp', split_axis=0, concat_axis=2, tiled=True)]
    ppermute x0 -> x30, starting transfers between devices: none -> 17.9 us  [the longest x6 8.39 us: all_gather_sp(): got = lax.ppermute(piece, 'sp', perm)]
    dot_general x19 -> x14, matrix products: 57.3 us -> 42.8 us  [the longest x4 17.4 us: shards(): jnp.dot(hidden, w_down[c * hid:(c + 1) * hid], preferred_element_type=F32)]
  transfers between devices with their start and end apart: 10 -> 34, of which waited for: 9 -> 15; matrix products, arithmetic and copies ran while one was open for 7% -> 10% of each run, Pallas kernels for 0% -> 0%
where the time goes in v1:
time: 563 us; the launch traced here: 558 us
  waiting for transfers between devices  374 us (66%)
  blocking collectives  50.2 us (9%)
  matrix products  44.7 us (8%)
  local copies, waits for them, and re-layouts  33.8 us (6%)
  other arithmetic  22.6 us (4%)
  starting transfers between devices  18.5 us (3%)
  between operations  14.1 us (3%)
    all_gather x2, waiting for transfers between devices, spread_rows(): whole = lax.all_gather(own, 'tp', axis=0, tiled=True)  128 us
    reduce_scatter x1, waiting for transfers between devices, shards(): lax.psum_scatter(mlp_part, 'tp', scatter_dimension=0, tiled=False)  79.9 us
    reduce_scatter x1, waiting for transfers between devices, shards(): lax.psum_scatter(attn_part, 'tp', scatter_dimension=0, tiled=False)  77.9 us
    ppermute x6, waiting for transfers between devices, reduce_scatter_sp(): total = total + lax.ppermute(piece, 'sp', perm).astype(F32)  46.6 us
    ppermute x6, waiting for transfers between devices, all_gather_sp(): got = lax.ppermute(piece, 'sp', perm)  40.4 us
    dot_general x4, matrix products, shards(): jnp.dot(hidden, w_down[c * hid:(c + 1) * hid], preferred_element_type=F32)  17.4 us
    all_to_all x1, blocking collectives, shards(): lax.all_to_all(block, 'tp', split_axis=2, concat_axis=0, tiled=False)  17.3 us
    all_to_all x1, blocking collectives, shards(): both = lax.all_to_all(both, 'sp', split_axis=3, concat_axis=2, tiled=False)  17.1 us
  transfers between devices with their start and end apart: 34, of which 15 were waited for; matrix products, arithmetic and copies ran while one was open for 10% of the time, Pallas kernels for 0%

profile of v1, /device:TPU:0, one launch (start us, length us, event | category | flops | bytes accessed | tf_op | source)
XLA Modules:
  0.0 558.2 jit_solution(7016403345779410773)
XLA Ops:
  6.5 1.1 slice_add_fusion
  7.6 5.8 %copy.100 = bf16[8,55,4096]{2,1,0:T(8,128)(2,1)} copy(bf16[8,55,4096]{2,0,1:T(8,128)(2,1)} %param.6) | data formatting | bytes 7208960 | tf_op args[0]
  13.4 1.2 convert_reduce_fusion.1
  16.8 17.1 %all_to_all.45 = bf16[2,1,1,56,4,1024]{5,3,2,1,0,4:T(8,128)(2,1)S(1)} all-to-all(bf16[2,1,1,56,4,1024]{5,3,2,1,0,4:T(8,128)(2,1)S(1)} %copy.101), channel_id=1, replica_groups=mesh['sp'=4,'tp'=8] {'sp'}, dimensions={4} | all-to-all | bytes 1835008 | tf_op jit(solution)/shard_map/all_to_all | solution.py:89
  33.9 1.3 fusion.105
  35.5 4.6 copy.103
  40.2 61.7 %all-gather.5.cloned.1.call-done = bf16[1792,1024]{1,0:T(8,128)(2,1)} async-done(((bf16[224,1024]{1,0:T(8,128)(2,1)}), bf16[1792,1024]{1,0:T(8,128)(2,1)}) %all-gather.5.cloned.1.call-update) | async-done | bytes 3670032 | tf_op jit(solution)/shard_map/all_gather | solution.py:162
  101.9 5.6 %convolution_convert_fusion.1 = bf16[896,1536]{1,0:T(8,128)(2,1)S(1)} fusion(bf16[1024,1536]{0,1:T(8,128)(2,1)} %bitcast.294, bf16[1792,1024]{1,0:T(8,128)(2,1)} %all-gather.5.cloned.1.call-done), kind=kOutput, calls=%fused_computation.6 | convolution fusion | flops 2819948544 | bytes 7733248 | tf_op jit(solution)/shard_map/dot_general | solution.py:106
  107.5 1.3 dynamic-slice_bitcast_fusion.1
  109.5 3.3 convolution_convert_fusion
  112.9 1.5 copy-done.4
  115.1 2.2 fusion.3
  117.4 1.5 collective-permute-start.1
  119.0 1.7 fusion.2
  122.1 13.7 %collective-permute-done.1 = bf16[224,1536]{1,0:T(8,128)(2,1)S(1)} collective-permute-done((bf16[224,1536]{1,0:T(8,128)(2,1)S(1)}, bf16[224,1536]{1,0:T(8,128)(2,1)S(1)}, u32[]{:S(2)}, u32[]{:S(2)}) %collective-permute-start.1) | collective-permute-done | bytes 688160 | tf_op jit(solution)/shard_map/ppermute | solution.py:37
  135.8 1.0 fusion.13
  136.8 2.4 reshape.270
  139.2 2.0 copy.145
  141.2 1.5 fusion.108
  142.7 2.5 fusion.18
  145.2 1.7 copy.107
  147.0 1.7 broadcast_in_dim_reshape.8
  148.7 1.7 copy.147
  150.4 1.5 collective-permute-start.3
  151.8 2.1 fusion.12
  154.0 2.2 reshape.273
  159.1 6.7 %collective-permute-done.8 = bf16[224,512]{1,0:T(8,128)(2,1)S(1)} collective-permute-done((bf16[224,512]{1,0:T(8,128)(2,1)S(1)}, bf16[224,512]{1,0:T(8,128)(2,1)S(1)}, u32[]{:S(2)}, u32[]{:S(2)}) %collective-permute-start.8) | collective-permute-done | bytes 229408 | tf_op jit(solution)/shard_map/ppermute | solution.py:52
  166.7 1.0 bitcast_dynamic-update-slice_fusion.20
  167.8 1.1 convolution_convert_fusion.7
  169.0 1.1 convolution_convert_fusion.6
  170.1 2.2 pad_maximum_fusion
  172.4 1.0 fusion.106
  173.4 77.9 %reduce-scatter.3.cloned.1.call-done = bf16[1,224,1024]{2,1,0:T(8,128)(2,1)} async-done(((bf16[8,224,1024]{2,1,0:T(8,128)(2,1)}), bf16[1,224,1024]{2,1,0:T(8,128)(2,1)}) %reduce-scatter.3.cloned.1.call-update) | async-done | bytes 458768 | tf_op jit(solution)/shard_map/reduce_scatter | solution.py:122
  251.3 1.1 convert_element_type.392
  253.1 5.2 all-gather.1
  258.4 2.2 add_convert_fusion.1
  260.8 65.9 %all-gather.7.cloned.1.call-done = bf16[1792,1024]{1,0:T(8,128)(2,1)} async-done(((bf16[224,1024]{1,0:T(8,128)(2,1)}), bf16[1792,1024]{1,0:T(8,128)(2,1)}) %all-gather.7.cloned.1.call-update) | async-done | bytes 3670032 | tf_op jit(solution)/shard_map/all_gather | solution.py:162
  326.7 4.5 convolution_convert_fusion.2
  331.5 2.2 convolution_convert_fusion.3
  334.2 2.2 convolution_convert_fusion.5
  336.6 2.2 convolution_convert_fusion.4
  339.7 1.5 collective-permute-start.26
  342.4 1.5 collective-permute-start.11
  344.9 8.2 %collective-permute-done.26 = bf16[448,512]{1,0:T(8,128)(2,1)S(1)} collective-permute-done((bf16[448,512]{1,0:T(8,128)(2,1)S(1)}, bf16[448,512]{1,0:T(8,128)(2,1)S(1)}, u32[]{:S(2)}, u32[]{:S(2)}) %collective-permute-start.26) | collective-permute-done | bytes 458784 | tf_op jit(solution)/shard_map/ppermute | solution.py:37
  353.7 1.5 collective-permute-start.28
  355.3 7.7 %collective-permute-done.21 = bf16[448,512]{1,0:T(8,128)(2,1)S(1)} collective-permute-done((bf16[448,512]{1,0:T(8,128)(2,1)S(1)}, bf16[448,512]{1,0:T(8,128)(2,1)S(1)}, u32[]{:S(2)}, u32[]{:S(2)}) %collective-permute-start.21) | collective-permute-done | bytes 458784 | tf_op jit(solution)/shard_map/ppermute | solution.py:37
  363.6 9.2 %collective-permute-done.11 = bf16[448,512]{1,0:T(8,128)(2,1)S(1)} collective-permute-done((bf16[448,512]{1,0:T(8,128)(2,1)S(1)}, bf16[448,512]{1,0:T(8,128)(2,1)S(1)}, u32[]{:S(2)}, u32[]{:S(2)}) %collective-permute-start.11) | collective-permute-done | bytes 458784 | tf_op jit(solution)/shard_map/ppermute | solution.py:37
  372.8 1.5 collective-permute-start.23
  374.8 7.8 %collective-permute-done.16 = bf16[448,512]{1,0:T(8,128)(2,1)S(1)} collective-permute-done((bf16[448,512]{1,0:T(8,128)(2,1)S(1)}, bf16[448,512]{1,0:T(8,128)(2,1)S(1)}, u32[]{:S(2)}, u32[]{:S(2)}) %collective-permute-start.16) | collective-permute-done | bytes 458784 | tf_op jit(solution)/shard_map/ppermute | solution.py:37
  383.2 1.7 collective-permute-start.13
  384.9 7.5 %collective-permute-done.28 = bf16[448,512]{1,0:T(8,128)(2,1)S(1)} collective-permute-done((bf16[448,512]{1,0:T(8,128)(2,1)S(1)}, bf16[448,512]{1,0:T(8,128)(2,1)S(1)}, u32[]{:S(2)}, u32[]{:S(2)}) %collective-permute-start.28) | collective-permute-done | bytes 458784 | tf_op jit(solution)/shard_map/ppermute | solution.py:52
  392.5 1.5 collective-permute-start.18
  394.1 8.2 %collective-permute-done.23 = bf16[448,512]{1,0:T(8,128)(2,1)S(1)} collective-permute-done((bf16[448,512]{1,0:T(8,128)(2,1)S(1)}, bf16[448,512]{1,0:T(8,128)(2,1)S(1)}, u32[]{:S(2)}, u32[]{:S(2)}) %collective-permute-start.23) | collective-permute-done | bytes 458784 | tf_op jit(solution)/shard_map/ppermute | solution.py:52
  402.9 9.2 %collective-permute-done.13 = bf16[448,512]{1,0:T(8,128)(2,1)S(1)} collective-permute-done((bf16[448,512]{1,0:T(8,128)(2,1)S(1)}, bf16[448,512]{1,0:T(8,128)(2,1)S(1)}, u32[]{:S(2)}, u32[]{:S(2)}) %collective-permute-start.13) | collective-permute-done | bytes 458784 | tf_op jit(solution)/shard_map/ppermute | solution.py:52
  412.1 8.9 %collective-permute-done.18 = bf16[448,512]{1,0:T(8,128)(2,1)S(1)} collective-permute-done((bf16[448,512]{1,0:T(8,128)(2,1)S(1)}, bf16[448,512]{1,0:T(8,128)(2,1)S(1)}, u32[]{:S(2)}, u32[]{:S(2)}) %collective-permute-start.18) | collective-permute-done | bytes 458784 | tf_op jit(solution)/shard_map/ppermute | solution.py:52
  421.2 1.6 collective-permute-done.19
  423.2 2.1 fusion.30
  425.3 2.1 fusion.33
  427.5 5.0 fusion.27
  432.5 8.2 %add_convert_fusion = bf16[1792,1024]{1,0:T(8,128)(2,1)} fusion(f32[1792,1024]{1,0:T(8,128)} %fusion.27, f32[1792,1024]{1,0:T(8,128)S(1)} %fusion.33, f32[1792,1024]{1,0:T(8,128)S(1)} %fusion.30, bf16[1792,512]{1,0:T(8,128)(2,1)S(1)} %bitcast.293, bf16[2048,1024]{1,0:T(8,128)(2,1)} %param.11), kind=kOutput, calls=%fused_computation.2 | convolution fusion | flops 1886388224 | bytes 28573696 | tf_op jit(solution)/shard_map/dot_general | solution.py:145
  440.8 79.9 %reduce-scatter.5.cloned.1.call-done = bf16[1,224,1024]{2,1,0:T(8,128)(2,1)} async-done(((bf16[8,224,1024]{2,1,0:T(8,128)(2,1)}), bf16[1,224,1024]{2,1,0:T(8,128)(2,1)}) %reduce-scatter.5.cloned.1.call-update) | async-done | bytes 458768 | tf_op jit(solution)/shard_map/reduce_scatter | solution.py:148
  520.7 1.2 fusion.79
  521.9 10.6 %all_to_all.46 = bf16[1,4,56,1,1024]{4,2,3,0,1:T(8,128)(2,1)S(1)} all-to-all(bf16[1,4,56,1,1024]{4,2,3,0,1:T(8,128)(2,1)S(1)} %fusion.79), channel_id=1, replica_groups=mesh['sp'=4,'tp'=8] {'sp'}, dimensions={1} | all-to-all | bytes 917504 | tf_op jit(solution)/shard_map/all_to_all | solution.py:152
  533.2 17.3 %all_to_all.47 = bf16[1,1,56,8,512]{4,2,1,0,3:T(8,128)(2,1)S(1)} all-to-all(bf16[1,1,56,8,512]{4,2,1,0,3:T(8,128)(2,1)S(1)} %copy.123), channel_id=1, replica_groups=mesh['sp'=4,'tp'=8] {'tp'}, dimensions={3} | all-to-all | bytes 917504 | tf_op jit(solution)/shard_map/all_to_all | solution.py:155
  (146 shorter events, 19.6 us)
Async XLA Ops:
  6.5 161.3 %copy-start = (bf16[512,1024]{1,0:T(8,128)(2,1)S(1)}, bf16[512,1024]{1,0:T(8,128)(2,1)}, u32[]{:S(2)}) copy-start(bf16[512,1024]{1,0:T(8,128)(2,1)} %param.9) | copy-start | bytes 3145732
  6.5 95.3 %all-gather.5.cloned.1.call-start = ((), (), s32[]{:S(2)}) async-start(), calls=%async_computation.5 | async-start | bytes 4128768 | tf_op jit(solution)/shard_map/all_gather | solution.py:162
  35.2 216.1 %reduce-scatter.3.cloned.1.call-start = ((), (), s32[]{:S(2)}) async-start(), calls=%async_computation.6 | async-start | bytes 4128768 | tf_op jit(solution)/shard_map/reduce_scatter | solution.py:122
  101.9 7.7 %copy-start.3 = (bf16[1024,3,512]{0,2,1:T(8,128)(2,1)S(1)}, bf16[1024,3,512]{0,2,1:T(8,128)(2,1)}, u32[]{:S(2)}) copy-start(bf16[1024,3,512]{0,2,1:T(8,128)(2,1)} %copy.103) | copy-start | bytes 9437188
  101.9 7.7 %copy-start.10 = (bf16[1792,1024]{1,0:T(8,128)(2,1)S(1)}, bf16[1792,1024]{1,0:T(8,128)(2,1)}, u32[]{:S(2)}) copy-start(bf16[1792,1024]{1,0:T(8,128)(2,1)} %all-gather.5.cloned.1.call-done) | copy-start | bytes 11010052
  107.5 2.0 copy-start.6
  109.5 5.6 collective-permute-start
  112.9 1.6 copy-start.4
  114.5 4.4 collective-permute-start.5
  115.1 3.9 copy-start.5
  117.4 18.4 %collective-permute-start.1 = (bf16[224,1536]{1,0:T(8,128)(2,1)S(1)}, bf16[224,1536]{1,0:T(8,128)(2,1)S(1)}, u32[]{:S(2)}, u32[]{:S(2)}) collective-permute-start(bf16[224,1536]{1,0:T(8,128)(2,1)S(1)} %dynamic-slice_bitcast_fusion.7), channel_id=1, source_target_pairs={{0,16},{8,24},{16,0},{24,8},{1,17},{9,25},{17,1},{25,9},{2,18},{10... | collective-permute-start | bytes 2064392 | tf_op jit(solution)/shard_map/ppermute | solution.py:37
  121.5 30.3 %collective-permute-start.6 = (bf16[224,1536]{1,0:T(8,128)(2,1)}, bf16[224,1536]{1,0:T(8,128)(2,1)}, u32[]{:S(2)}, u32[]{:S(2)}) collective-permute-start(bf16[224,1536]{1,0:T(8,128)(2,1)} %dynamic-slice_bitcast_fusion.6), channel_id=1, source_target_pairs={{0,16},{8,24},{16,0},{24,8},{1,17},{9,25},{17,1},{25,9},{2,18},{10... | collective-permute-start | bytes 2064392 | tf_op jit(solution)/shard_map/ppermute | solution.py:37
  150.4 8.4 %collective-permute-start.3 = (bf16[224,512]{1,0:T(8,128)(2,1)}, bf16[224,512]{1,0:T(8,128)(2,1)}, u32[]{:S(2)}, u32[]{:S(2)}) collective-permute-start(bf16[224,512]{1,0:T(8,128)(2,1)} %bitcast.284), channel_id=1, source_target_pairs={{0,16},{8,24},{16,0},{24,8},{1,17},{9,25},{17,1},{25,9},{2,18},{10... | collective-permute-start | bytes 688136 | tf_op jit(solution)/shard_map/ppermute | solution.py:52
  151.8 13.9 %collective-permute-start.2 = (bf16[224,512]{1,0:T(8,128)(2,1)}, bf16[224,512]{1,0:T(8,128)(2,1)}, u32[]{:S(2)}, u32[]{:S(2)}) collective-permute-start(bf16[224,512]{1,0:T(8,128)(2,1)} %bitcast.284), channel_id=1, source_target_pairs={{0,8},{8,0},{16,24},{24,16},{1,9},{9,1},{17,25},{25,17},{2,10},{10... | collective-permute-start | bytes 688136 | tf_op jit(solution)/shard_map/ppermute | solution.py:53
  157.4 1.2 copy-start.7
  157.7 8.1 %collective-permute-start.8 = (bf16[224,512]{1,0:T(8,128)(2,1)S(1)}, bf16[224,512]{1,0:T(8,128)(2,1)S(1)}, u32[]{:S(2)}, u32[]{:S(2)}) collective-permute-start(bf16[224,512]{1,0:T(8,128)(2,1)S(1)} %bitcast.323), channel_id=1, source_target_pairs={{0,16},{8,24},{16,0},{24,8},{1,17},{9,25},{17,1},{25,9},{2,18},{10... | collective-permute-start | bytes 688136 | tf_op jit(solution)/shard_map/ppermute | solution.py:52
  158.3 9.4 %collective-permute-start.7 = (bf16[224,512]{1,0:T(8,128)(2,1)S(1)}, bf16[224,512]{1,0:T(8,128)(2,1)S(1)}, u32[]{:S(2)}, u32[]{:S(2)}) collective-permute-start(bf16[224,512]{1,0:T(8,128)(2,1)S(1)} %bitcast.324), channel_id=1, source_target_pairs={{0,8},{8,0},{16,24},{24,16},{1,9},{9,1},{17,25},{25,17},{2,10},{10... | collective-permute-start | bytes 688136 | tf_op jit(solution)/shard_map/ppermute | solution.py:53
  158.8 9.0 %collective-permute-start.4 = (bf16[224,512]{1,0:T(8,128)(2,1)}, bf16[224,512]{1,0:T(8,128)(2,1)S(1)}, u32[]{:S(2)}, u32[]{:S(2)}) collective-permute-start(bf16[224,512]{1,0:T(8,128)(2,1)} %collective-permute-done.3), channel_id=1, source_target_pairs={{0,8},{8,0},{16,24},{24,16},{1,9},{9,1},{17,25},{25,17},{2,10},{10... | collective-permute-start | bytes 688136 | tf_op jit(solution)/shard_map/ppermute | solution.py:53
  165.8 3.2 collective-permute-start.9
  172.3 154.4 %all-gather.7.cloned.1.call-start = ((), (), s32[]{:S(2)}) async-start(), calls=%async_computation.7 | async-start | bytes 4128768 | tf_op jit(solution)/shard_map/all_gather | solution.py:162
  173.4 85.0 %copy-start.2 = (f32[1,1,4,1,56,1,1024]{6,4,2,5,3,1,0:T(8,128)S(1)}, f32[1,1,4,1,56,1,1024]{6,4,2,5,3,1,0:T(8,128)}, u32[]{:S(2)}) copy-start(f32[1,1,4,1,56,1,1024]{6,4,2,5,3,1,0:T(8,128)} %get-tuple-element.20) | copy-start | bytes 2752516
  260.6 260.1 %reduce-scatter.5.cloned.1.call-start = ((), (), s32[]{:S(2)}) async-start(), calls=%async_computation.8 | async-start | bytes 4128768 | tf_op jit(solution)/shard_map/reduce_scatter | solution.py:148
  326.7 4.7 copy-start.9
  326.7 4.7 copy-start.11
  331.3 8.0 %collective-permute-start.25 = (bf16[2,448,512]{2,1,0:T(8,128)(2,1)S(1)}, bf16[2,448,512]{2,1,0:T(8,128)(2,1)S(1)}, u32[]{:S(2)}, u32[]{:S(2)}) collective-permute-start(bf16[2,448,512]{2,1,0:T(8,128)(2,1)S(1)} %dynamic-slice_bitcast_fusion.2), channel_id=1, source_target_pairs={{0,8},{8,0},{16,24},{24,16},{1,9},{9,1},{17,25},{25,17},{2,10},{10... | collective-permute-start | bytes 2752520 | tf_op jit(solution)/shard_map/ppermute | solution.py:30
  333.7 7.5 %collective-permute-start.20 = (bf16[2,448,512]{2,1,0:T(8,128)(2,1)S(1)}, bf16[2,448,512]{2,1,0:T(8,128)(2,1)S(1)}, u32[]{:S(2)}, u32[]{:S(2)}) collective-permute-start(bf16[2,448,512]{2,1,0:T(8,128)(2,1)S(1)} %dynamic-slice_bitcast_fusion.3), channel_id=1, source_target_pairs={{0,8},{8,0},{16,24},{24,16},{1,9},{9,1},{17,25},{25,17},{2,10},{10... | collective-permute-start | bytes 2752520 | tf_op jit(solution)/shard_map/ppermute | solution.py:30
  336.5 5.6 %collective-permute-start.10 = (bf16[2,448,512]{2,1,0:T(8,128)(2,1)S(1)}, bf16[2,448,512]{2,1,0:T(8,128)(2,1)S(1)}, u32[]{:S(2)}, u32[]{:S(2)}) collective-permute-start(bf16[2,448,512]{2,1,0:T(8,128)(2,1)S(1)} %dynamic-slice_bitcast_fusion.5), channel_id=1, source_target_pairs={{0,8},{8,0},{16,24},{24,16},{1,9},{9,1},{17,25},{25,17},{2,10},{10... | collective-permute-start | bytes 2752520 | tf_op jit(solution)/shard_map/ppermute | solution.py:30
  338.8 5.1 collective-permute-start.15
  339.7 13.5 %collective-permute-start.26 = (bf16[448,512]{1,0:T(8,128)(2,1)S(1)}, bf16[448,512]{1,0:T(8,128)(2,1)S(1)}, u32[]{:S(2)}, u32[]{:S(2)}) collective-permute-start(bf16[448,512]{1,0:T(8,128)(2,1)S(1)} %dynamic-slice_bitcast_fusion.8), channel_id=1, source_target_pairs={{0,16},{8,24},{16,0},{24,8},{1,17},{9,25},{17,1},{25,9},{2,18},{10... | collective-permute-start | bytes 1376264 | tf_op jit(solution)/shard_map/ppermute | solution.py:37
  341.5 21.4 %collective-permute-start.21 = (bf16[448,512]{1,0:T(8,128)(2,1)S(1)}, bf16[448,512]{1,0:T(8,128)(2,1)S(1)}, u32[]{:S(2)}, u32[]{:S(2)}) collective-permute-start(bf16[448,512]{1,0:T(8,128)(2,1)S(1)} %dynamic-slice_bitcast_fusion.9), channel_id=1, source_target_pairs={{0,16},{8,24},{16,0},{24,8},{1,17},{9,25},{17,1},{25,9},{2,18},{10... | collective-permute-start | bytes 1376264 | tf_op jit(solution)/shard_map/ppermute | solution.py:37
  342.4 30.4 %collective-permute-start.11 = (bf16[448,512]{1,0:T(8,128)(2,1)S(1)}, bf16[448,512]{1,0:T(8,128)(2,1)S(1)}, u32[]{:S(2)}, u32[]{:S(2)}) collective-permute-start(bf16[448,512]{1,0:T(8,128)(2,1)S(1)} %dynamic-slice_bitcast_fusion.11), channel_id=1, source_target_pairs={{0,16},{8,24},{16,0},{24,8},{1,17},{9,25},{17,1},{25,9},{2,18},{10... | collective-permute-start | bytes 1376264 | tf_op jit(solution)/shard_map/ppermute | solution.py:37
  344.3 38.3 %collective-permute-start.16 = (bf16[448,512]{1,0:T(8,128)(2,1)S(1)}, bf16[448,512]{1,0:T(8,128)(2,1)S(1)}, u32[]{:S(2)}, u32[]{:S(2)}) collective-permute-start(bf16[448,512]{1,0:T(8,128)(2,1)S(1)} %dynamic-slice_bitcast_fusion.10), channel_id=1, source_target_pairs={{0,16},{8,24},{16,0},{24,8},{1,17},{9,25},{17,1},{25,9},{2,18},{10... | collective-permute-start | bytes 1376264 | tf_op jit(solution)/shard_map/ppermute | solution.py:37
  353.7 29.5 %collective-permute-start.27 = (bf16[448,512]{1,0:T(8,128)(2,1)S(1)}, bf16[448,512]{1,0:T(8,128)(2,1)S(1)}, u32[]{:S(2)}, u32[]{:S(2)}) collective-permute-start(bf16[448,512]{1,0:T(8,128)(2,1)S(1)} %get-tuple-element.8), channel_id=1, source_target_pairs={{0,8},{8,0},{16,24},{24,16},{1,9},{9,1},{17,25},{25,17},{2,10},{10... | collective-permute-start | bytes 1376264 | tf_op jit(solution)/shard_map/ppermute | solution.py:53
  353.7 38.7 %collective-permute-start.28 = (bf16[448,512]{1,0:T(8,128)(2,1)S(1)}, bf16[448,512]{1,0:T(8,128)(2,1)S(1)}, u32[]{:S(2)}, u32[]{:S(2)}) collective-permute-start(bf16[448,512]{1,0:T(8,128)(2,1)S(1)} %get-tuple-element.8), channel_id=1, source_target_pairs={{0,16},{8,24},{16,0},{24,8},{1,17},{9,25},{17,1},{25,9},{2,18},{10... | collective-permute-start | bytes 1376264 | tf_op jit(solution)/shard_map/ppermute | solution.py:52
  363.5 29.0 %collective-permute-start.22 = (bf16[448,512]{1,0:T(8,128)(2,1)S(1)}, bf16[448,512]{1,0:T(8,128)(2,1)S(1)}, u32[]{:S(2)}, u32[]{:S(2)}) collective-permute-start(bf16[448,512]{1,0:T(8,128)(2,1)S(1)} %get-tuple-element.14), channel_id=1, source_target_pairs={{0,8},{8,0},{16,24},{24,16},{1,9},{9,1},{17,25},{25,17},{2,10},{10... | collective-permute-start | bytes 1376264 | tf_op jit(solution)/shard_map/ppermute | solution.py:53
  372.8 29.5 %collective-permute-start.23 = (bf16[448,512]{1,0:T(8,128)(2,1)S(1)}, bf16[448,512]{1,0:T(8,128)(2,1)S(1)}, u32[]{:S(2)}, u32[]{:S(2)}) collective-permute-start(bf16[448,512]{1,0:T(8,128)(2,1)S(1)} %get-tuple-element.14), channel_id=1, source_target_pairs={{0,16},{8,24},{16,0},{24,8},{1,17},{9,25},{17,1},{25,9},{2,18},{10... | collective-permute-start | bytes 1376264 | tf_op jit(solution)/shard_map/ppermute | solution.py:52
  382.6 19.7 %collective-permute-start.12 = (bf16[448,512]{1,0:T(8,128)(2,1)S(1)}, bf16[448,512]{1,0:T(8,128)(2,1)S(1)}, u32[]{:S(2)}, u32[]{:S(2)}) collective-permute-start(bf16[448,512]{1,0:T(8,128)(2,1)S(1)} %get-tuple-element.12), channel_id=1, source_target_pairs={{0,8},{8,0},{16,24},{24,16},{1,9},{9,1},{17,25},{25,17},{2,10},{10... | collective-permute-start | bytes 1376264 | tf_op jit(solution)/shard_map/ppermute | solution.py:53
  383.2 28.9 %collective-permute-start.13 = (bf16[448,512]{1,0:T(8,128)(2,1)S(1)}, bf16[448,512]{1,0:T(8,128)(2,1)S(1)}, u32[]{:S(2)}, u32[]{:S(2)}) collective-permute-start(bf16[448,512]{1,0:T(8,128)(2,1)S(1)} %get-tuple-element.12), channel_id=1, source_target_pairs={{0,16},{8,24},{16,0},{24,8},{1,17},{9,25},{17,1},{25,9},{2,18},{10... | collective-permute-start | bytes 1376264 | tf_op jit(solution)/shard_map/ppermute | solution.py:52
  392.4 28.7 %collective-permute-start.17 = (bf16[448,512]{1,0:T(8,128)(2,1)S(1)}, bf16[448,512]{1,0:T(8,128)(2,1)S(1)}, u32[]{:S(2)}, u32[]{:S(2)}) collective-permute-start(bf16[448,512]{1,0:T(8,128)(2,1)S(1)} %get-tuple-element.10), channel_id=1, source_target_pairs={{0,8},{8,0},{16,24},{24,16},{1,9},{9,1},{17,25},{25,17},{2,10},{10... | collective-permute-start | bytes 1376264 | tf_op jit(solution)/shard_map/ppermute | solution.py:53
  392.5 28.5 %collective-permute-start.18 = (bf16[448,512]{1,0:T(8,128)(2,1)S(1)}, bf16[448,512]{1,0:T(8,128)(2,1)S(1)}, u32[]{:S(2)}, u32[]{:S(2)}) collective-permute-start(bf16[448,512]{1,0:T(8,128)(2,1)S(1)} %get-tuple-element.10), channel_id=1, source_target_pairs={{0,16},{8,24},{16,0},{24,8},{1,17},{9,25},{17,1},{25,9},{2,18},{10... | collective-permute-start | bytes 1376264 | tf_op jit(solution)/shard_map/ppermute | solution.py:52
  402.3 30.2 %collective-permute-start.29 = (bf16[448,512]{1,0:T(8,128)(2,1)S(1)}, bf16[448,512]{1,0:T(8,128)(2,1)S(1)}, u32[]{:S(2)}, u32[]{:S(2)}) collective-permute-start(bf16[448,512]{1,0:T(8,128)(2,1)S(1)} %collective-permute-done.28), channel_id=1, source_target_pairs={{0,8},{8,0},{16,24},{24,16},{1,9},{9,1},{17,25},{25,17},{2,10},{10... | collective-permute-start | bytes 1376264 | tf_op jit(solution)/shard_map/ppermute | solution.py:53
  402.3 25.1 %collective-permute-start.24 = (bf16[448,512]{1,0:T(8,128)(2,1)S(1)}, bf16[448,512]{1,0:T(8,128)(2,1)S(1)}, u32[]{:S(2)}, u32[]{:S(2)}) collective-permute-start(bf16[448,512]{1,0:T(8,128)(2,1)S(1)} %collective-permute-done.23), channel_id=1, source_target_pairs={{0,8},{8,0},{16,24},{24,16},{1,9},{9,1},{17,25},{25,17},{2,10},{10... | collective-permute-start | bytes 1376264 | tf_op jit(solution)/shard_map/ppermute | solution.py:53
  412.1 13.2 %collective-permute-start.14 = (bf16[448,512]{1,0:T(8,128)(2,1)S(1)}, bf16[448,512]{1,0:T(8,128)(2,1)S(1)}, u32[]{:S(2)}, u32[]{:S(2)}) collective-permute-start(bf16[448,512]{1,0:T(8,128)(2,1)S(1)} %collective-permute-done.13), channel_id=1, source_target_pairs={{0,8},{8,0},{16,24},{24,16},{1,9},{9,1},{17,25},{25,17},{2,10},{10... | collective-permute-start | bytes 1376264 | tf_op jit(solution)/shard_map/ppermute | solution.py:53
  421.0 1.8 collective-permute-start.19
  421.0 2.2 copy-start.8
  532.6 18.9 %copy-start.1 = (bf16[512,1024]{1,0:T(8,128)(2,1)S(1)}, bf16[512,1024]{1,0:T(8,128)(2,1)}, u32[]{:S(2)}) copy-start(bf16[512,1024]{1,0:T(8,128)(2,1)} %param.9) | copy-start | bytes 3145732
Sparse Core Ops, SparseCore 0:
  35.3 66.5 all-gather.4
  172.4 78.8 reduce-scatter.2
  260.7 65.9 all-gather.6
  440.9 79.7 reduce-scatter.4

commit v2 on v1

--- a/solution.py
+++ b/solution.py
@@ -85,10 +85,13 @@
         padded_tokens, ((tp_me // sub) * f_own, (tp_me % sub) * part, 0), (f_own, part, width)
     )
     mod_mine = normalize(mine, modulation[0], modulation[1])
-    both = jnp.stack([mod_mine, mine]).reshape(2, f_own, part, sp_count, slab)
-    both = lax.all_to_all(both, "sp", split_axis=3, concat_axis=2, tiled=False)
-    mod_slab = both[0].reshape(own_rows, slab)
-    tok_slab = both[1].reshape(own_rows, slab)
+    def to_slabs(value):
+        value = value.reshape(f_own * part, sp_count, slab)
+        value = exchange(jnp.transpose(value, (1, 0, 2)), "sp")
+        value = value.reshape(sp_count, f_own, part, slab)
+        return jnp.transpose(value, (1, 0, 2, 3)).reshape(own_rows, slab)
+
+    mod_slab, tok_slab = to_slabs(mod_mine), to_slabs(mine)
     mod_a = spread_rows(mod_slab, frames, sub, f_own, rows)
 
     at = jnp.arange(rows)
@@ -119,7 +122,7 @@
         att = att.reshape(f_chunk * rows, heads * DH)
         attn_parts.append(jnp.dot(att, w_out, preferred_element_type=F32).astype(BF))
     attn_part = jnp.concatenate(attn_parts, 0).reshape(tp_count, own_rows, slab)
-    attn_sum = lax.psum_scatter(attn_part, "tp", scatter_dimension=0, tiled=False).astype(F32)
+    attn_sum = reduce_scatter_tp(attn_part)
 
     mod_slice = lax.dynamic_slice_in_dim(modulation, sp_me * slab, slab, 1)
     middle = (tok_slab.astype(F32) + mod_slice[2] * attn_sum).astype(BF)
@@ -145,22 +148,108 @@
         term = jnp.dot(hidden, w_down[c * hid : (c + 1) * hid], preferred_element_type=F32)
         acc = term if acc is None else acc + term
     mlp_part = acc.astype(BF).reshape(tp_count, own_rows, slab)
-    mlp_sum = lax.psum_scatter(mlp_part, "tp", scatter_dimension=0, tiled=False).astype(F32)
+    mlp_sum = reduce_scatter_tp(mlp_part)
     block = (middle.astype(F32) + mod_slice[5] * mlp_sum).astype(BF)
 
-    block = block.reshape(f_own, sp_count, part, slab)
-    block = lax.all_to_all(block, "sp", split_axis=1, concat_axis=2, tiled=False)
-    block = block.reshape(f_own, part, width)
-    block = block.reshape(f_own, part, tp_count, width // tp_count)
-    block = lax.all_to_all(block, "tp", split_axis=2, concat_axis=0, tiled=False)
+    block = jnp.transpose(block.reshape(f_own, sp_count, part, slab), (1, 0, 2, 3))
+    block = exchange(block.reshape(sp_count, f_own * part, slab), "sp")
+    block = jnp.transpose(block, (1, 0, 2)).reshape(f_own * part, tp_count, width // tp_count)
+    block = exchange(jnp.transpose(block, (1, 0, 2)), "tp")
     block = block.reshape(groups, sub, f_own, part, width // tp_count)
     block = jnp.transpose(block, (0, 2, 1, 3, 4)).reshape(frames, padded, width // tp_count)
     return block[:, :patches]
 
 
+def tp_grid():
+    count = lax.axis_size("tp")
+    lanes = 2 ** ((count.bit_length() - 1) // 2)
+    return count, count // lanes, lanes
+
+
+def ring_shift(value, k):
+    count, ring, lanes = tp_grid()
+    return lax.ppermute(
+        value, "tp", [(i, ((i // lanes + k) % ring) * lanes + i % lanes) for i in range(count)]
+    )
+
+
+def lane_shift(value, k):
+    count, ring, lanes = tp_grid()
+    return lax.ppermute(
+        value, "tp", [(i, (i // lanes) * lanes + (i + k) % lanes) for i in range(count)]
+    )
+
+
+def ring_pieces(piece):
+    ring = tp_grid()[1]
+    if ring != 4:
+        return [(k, ring_shift(piece, k) if k else piece) for k in range(ring)]
+    half = piece.shape[1] // 2
+    left, right = ring_shift(piece, 1), ring_shift(piece, -1)
+    far = [ring_shift(left[:, :half], 1), ring_shift(right[:, half:], -1)]
+    return [(0, piece), (1, left), (3, right), (2, jnp.concatenate(far, 1))]
+
+
+def ring_reduce(parts):
+    ring = parts.shape[0]
+    _, _, lanes = tp_grid()
+    place = lax.axis_index("tp") // lanes
+
+    def part(k):
+        return lax.dynamic_index_in_dim(parts, (place + k) % ring, 0, keepdims=False)
+
+    total = part(0).astype(F32)
+    if ring != 4:
+        for k in range(1, ring):
+            total = total + ring_shift(part(k), k).astype(F32)
+        return total
+    half = parts.shape[2] // 2
+    far = part(2)
+    from_left, from_right = ring_shift(far[:, :half], 1), ring_shift(far[:, half:], -1)
+    ahead, behind = part(1), part(3)
+    low = (ahead[:, :half].astype(F32) + from_left.astype(F32)).astype(BF)
+    high = (behind[:, half:].astype(F32) + from_right.astype(F32)).astype(BF)
+    ahead = jnp.concatenate([low, ahead[:, half:]], 1)
+    behind = jnp.concatenate([behind[:, :half], high], 1)
+    return total + ring_shift(ahead, 1).astype(F32) + ring_shift(behind, -1).astype(F32)
+
+
+def reduce_scatter_tp(parts):
+    count, ring, lanes = tp_grid()
+    lane = lax.axis_index("tp") % lanes
+    grid = parts.reshape((ring, lanes) + parts.shape[1:])
+    total = None
+    for k in list(range(1, lanes)) + [0]:
+        picked = lax.dynamic_index_in_dim(grid, (lane + k) % lanes, 1, keepdims=False)
+        summed = ring_reduce(picked)
+        if k:
+            summed = lane_shift(summed.astype(BF), k).astype(F32)
+        total = summed if total is None else total + summed
+    return total
+
+
 def spread_rows(own, frames, sub, f_own, rows):
-    whole = lax.all_gather(own, "tp", axis=0, tiled=True)
-    return whole.reshape(frames, rows, own.shape[1])
+    count, ring, lanes = tp_grid()
+    me = lax.axis_index("tp")
+    place, lane = me // lanes, me % lanes
+    out = jnp.zeros((count,) + own.shape, own.dtype)
+    for k in range(lanes):
+        column = lane_shift(own, k) if k else own
+        for back, piece in ring_pieces(column):
+            at = ((place - back) % ring) * lanes + (lane - k) % lanes
+            out = lax.dynamic_update_slice(out, piece[None], (at, 0, 0))
+    return out.reshape(frames, rows, own.shape[1])
+
+
+def exchange(parts, axis):
+    count = parts.shape[0]
+    me = lax.axis_index(axis)
+    out = parts
+    for k in range(1, count):
+        piece = lax.dynamic_index_in_dim(parts, (me + k) % count, 0)
+        got = lax.ppermute(piece, axis, [(i, (i + k) % count) for i in range(count)])
+        out = lax.dynamic_update_slice_in_dim(out, got, (me - k) % count, 0)
+    return out
 
 
 def solution(mesh):

time: 563 us -> 530 us (0.941)
  starting transfers between devices: 18.5 us -> 97.9 us
  waiting for transfers between devices: 374 us -> 295 us
  blocking collectives: 50.2 us -> 5.19 us
  local copies, waits for them, and re-layouts: 33.8 us -> 58.7 us
  between operations: 14.1 us -> 1.94 us
    ppermute x0 -> x52, waiting for transfers between devices: none -> 206 us  [the longest x32 187 us: ring_shift(): lax.ppermute(value, 'tp', [(i, (i // lanes + k) % ring * lanes + i % lane...]
    reduce_scatter x2 -> x0, waiting for transfers between devices: 158 us -> none  [the longest x1 79.9 us: shards(): lax.psum_scatter(mlp_part, 'tp', scatter_dimension=0, tiled=False)]
    all_gather x2 -> x0, waiting for transfers between devices: 128 us -> none  [spread_rows(): whole = lax.all_gather(own, 'tp', axis=0, tiled=True)]
    ppermute x0 -> x52, starting transfers between devices: none -> 78.7 us  [the longest x32 54.4 us: ring_shift(): lax.ppermute(value, 'tp', [(i, (i // lanes + k) % ring * lanes + i % lane...]
    all_to_all x3 -> x0, blocking collectives: 45 us -> none  [the longest x1 17.3 us: shards(): lax.all_to_all(block, 'tp', split_axis=2, concat_axis=0, tiled=False)]
    dynamic_update_slice x0 -> x27, local copies, waits for them, and re-layouts: none -> 23 us  [the longest x16 22.5 us: exchange(): out = lax.dynamic_update_slice_in_dim(out, got, (me - k) % count, 0)]
    unnamed x28 -> x31, local copies, waits for them, and re-layouts: 14.8 us -> 15.8 us
  transfers between devices with their start and end apart: 34 -> 82, of which waited for: 15 -> 47; matrix products, arithmetic and copies ran while one was open for 10% -> 15% of each run, Pallas kernels for 0% -> 0%
where the time goes in v2:
time: 530 us; the launch traced here: 521 us
  waiting for transfers between devices  295 us (56%)
  starting transfers between devices  97.9 us (18%)
  local copies, waits for them, and re-layouts  58.7 us (11%)
  matrix products  42 us (8%)
  other arithmetic  19.9 us (4%)
    ppermute x32, waiting for transfers between devices, ring_shift(): lax.ppermute(value, 'tp', [(i, (i // lanes + k) % ring * lanes + i % lane...  187 us
    ppermute x32, starting transfers between devices, ring_shift(): lax.ppermute(value, 'tp', [(i, (i // lanes + k) % ring * lanes + i % lane...  54.4 us
    ppermute x6, waiting for transfers between devices, reduce_scatter_sp(): total = total + lax.ppermute(piece, 'sp', perm).astype(F32)  49.1 us
    ppermute x6, waiting for transfers between devices, all_gather_sp(): got = lax.ppermute(piece, 'sp', perm)  39.9 us
    dynamic_update_slice x16, local copies, waits for them, and re-layouts, exchange(): out = lax.dynamic_update_slice_in_dim(out, got, (me - k) % count, 0)  22.5 us
    dot_general x4, matrix products, shards(): jnp.dot(hidden, w_down[c * hid:(c + 1) * hid], preferred_element_type=F32)  20.2 us
    ppermute x16, waiting for transfers between devices, exchange(): lax.ppermute(piece, axis, [(i, (i + k) % count) for i in range(count)])  19.1 us
    ppermute x16, starting transfers between devices, exchange(): lax.ppermute(piece, axis, [(i, (i + k) % count) for i in range(count)])  18.2 us
  transfers between devices with their start and end apart: 82, of which 47 were waited for; matrix products, arithmetic and copies ran while one was open for 15% of the time, Pallas kernels for 0%

profile of v2, /device:TPU:0, one launch (start us, length us, event | category | flops | bytes accessed | tf_op | source)
XLA Modules:
  0.0 520.7 jit_solution(2116081824539977933)
XLA Ops:
  0.0 5.9 %copy.91 = bf16[8,55,4096]{2,1,0:T(8,128)(2,1)} copy(bf16[8,55,4096]{2,0,1:T(8,128)(2,1)} %param.6) | data formatting | bytes 7208960 | tf_op args[0]
  12.0 2.5 collective-permute-start.4
  16.0 3.3 collective-permute-done.3
  31.9 4.7 copy.95
  37.1 3.9 collective-permute-done.6
  41.0 10.3 %collective-permute-done.7 = bf16[224,1024]{1,0:T(8,128)(2,1)S(1)} collective-permute-done((bf16[224,1024]{1,0:T(8,128)(2,1)S(1)}, bf16[224,1024]{1,0:T(8,128)(2,1)S(1)}, u32[]{:S(2)}, u32[]{:S(2)}) %collective-permute-start.7) | collective-permute-done | bytes 458784 | tf_op jit(solution)/shard_map/ppermute | solution.py:171
  53.4 2.9 collective-permute-start.12
  56.4 13.2 %collective-permute-done.9 = bf16[224,512]{1,0:T(8,128)(2,1)S(1)} collective-permute-done((bf16[224,512]{1,0:T(8,128)(2,1)S(1)}, bf16[224,512]{1,0:T(8,128)(2,1)S(1)}, u32[]{:S(2)}, u32[]{:S(2)}) %collective-permute-start.9) | collective-permute-done | bytes 229408 | tf_op jit(solution)/shard_map/ppermute | solution.py:171
  71.3 12.4 %collective-permute-done.12 = bf16[224,1024]{1,0:T(8,128)(2,1)S(1)} collective-permute-done((bf16[224,1024]{1,0:T(8,128)(2,1)S(1)}, bf16[224,1024]{1,0:T(8,128)(2,1)S(1)}, u32[]{:S(2)}, u32[]{:S(2)}) %collective-permute-start.12) | collective-permute-done | bytes 458784 | tf_op jit(solution)/shard_map/ppermute | solution.py:171
  83.9 7.3 %collective-permute-done.14 = bf16[224,512]{1,0:T(8,128)(2,1)S(1)} collective-permute-done((bf16[224,512]{1,0:T(8,128)(2,1)S(1)}, bf16[224,512]{1,0:T(8,128)(2,1)S(1)}, u32[]{:S(2)}, u32[]{:S(2)}) %collective-permute-start.14) | collective-permute-done | bytes 229408 | tf_op jit(solution)/shard_map/ppermute | solution.py:171
  93.2 3.3 convolution_convert_fusion.1
  98.4 3.3 convolution_convert_fusion
  111.9 13.1 %collective-permute-done.16 = bf16[224,1536]{1,0:T(8,128)(2,1)S(1)} collective-permute-done((bf16[224,1536]{1,0:T(8,128)(2,1)S(1)}, bf16[224,1536]{1,0:T(8,128)(2,1)S(1)}, u32[]{:S(2)}, u32[]{:S(2)}) %collective-permute-start.16) | collective-permute-done | bytes 688160 | tf_op jit(solution)/shard_map/ppermute | solution.py:37
  137.1 2.8 collective-permute-done.21
  148.1 5.8 %collective-permute-done.23 = bf16[224,512]{1,0:T(8,128)(2,1)S(1)} collective-permute-done((bf16[224,512]{1,0:T(8,128)(2,1)S(1)}, bf16[224,512]{1,0:T(8,128)(2,1)S(1)}, u32[]{:S(2)}, u32[]{:S(2)}) %collective-permute-start.23) | collective-permute-done | bytes 229408 | tf_op jit(solution)/shard_map/ppermute | solution.py:52
  163.1 3.9 collective-permute-start.32
  167.0 2.4 collective-permute-done.25
  169.6 4.8 collective-permute-done.27
  176.4 2.9 collective-permute-done.30
  180.2 4.0 collective-permute-done.32
  186.9 7.1 %collective-permute-done.26 = bf16[224,1024]{1,0:T(8,128)(2,1)S(1)} collective-permute-done((bf16[224,1024]{1,0:T(8,128)(2,1)S(1)}, bf16[224,1024]{1,0:T(8,128)(2,1)S(1)}, u32[]{:S(2)}, u32[]{:S(2)}) %collective-permute-start.26) | collective-permute-done | bytes 458784 | tf_op jit(solution)/shard_map/ppermute | solution.py:171
  194.1 9.8 %collective-permute-done.28 = bf16[224,1024]{1,0:T(8,128)(2,1)S(1)} collective-permute-done((bf16[224,1024]{1,0:T(8,128)(2,1)S(1)}, bf16[224,1024]{1,0:T(8,128)(2,1)S(1)}, u32[]{:S(2)}, u32[]{:S(2)}) %collective-permute-start.28) | collective-permute-done | bytes 458784 | tf_op jit(solution)/shard_map/ppermute | solution.py:171
  207.8 2.7 collective-permute-done.1
  210.6 3.2 collective-permute-done.31
  213.8 9.0 %collective-permute-done.33 = bf16[224,1024]{1,0:T(8,128)(2,1)S(1)} collective-permute-done((bf16[224,1024]{1,0:T(8,128)(2,1)}, bf16[224,1024]{1,0:T(8,128)(2,1)S(1)}, u32[]{:S(2)}, u32[]{:S(2)}) %collective-permute-start.33) | collective-permute-done | bytes 458784 | tf_op jit(solution)/shard_map/ppermute | solution.py:171
  224.7 5.2 all-gather.1
  231.1 3.5 collective-permute-start.35
  236.2 9.9 %collective-permute-done.34 = bf16[224,1024]{1,0:T(8,128)(2,1)S(1)} collective-permute-done((bf16[224,1024]{1,0:T(8,128)(2,1)S(1)}, bf16[224,1024]{1,0:T(8,128)(2,1)S(1)}, u32[]{:S(2)}, u32[]{:S(2)}) %collective-permute-start.34) | collective-permute-done | bytes 458784 | tf_op jit(solution)/shard_map/ppermute | solution.py:171
  246.1 7.3 %collective-permute-done.35 = bf16[224,1024]{1,0:T(8,128)(2,1)S(1)} collective-permute-done((bf16[224,1024]{1,0:T(8,128)(2,1)S(1)}, bf16[224,1024]{1,0:T(8,128)(2,1)S(1)}, u32[]{:S(2)}, u32[]{:S(2)}) %collective-permute-start.35) | collective-permute-done | bytes 458784 | tf_op jit(solution)/shard_map/ppermute | solution.py:171
  253.5 2.8 collective-permute-start.37
  256.3 3.8 collective-permute-start.40
  260.8 5.0 collective-permute-done.37
  265.9 9.7 %collective-permute-done.39 = bf16[224,1024]{1,0:T(8,128)(2,1)S(1)} collective-permute-done((bf16[224,1024]{1,0:T(8,128)(2,1)S(1)}, bf16[224,1024]{1,0:T(8,128)(2,1)S(1)}, u32[]{:S(2)}, u32[]{:S(2)}) %collective-permute-start.39) | collective-permute-done | bytes 458784 | tf_op jit(solution)/shard_map/ppermute | solution.py:171
  275.7 9.1 %collective-permute-done.40 = bf16[224,1024]{1,0:T(8,128)(2,1)S(1)} collective-permute-done((bf16[224,1024]{1,0:T(8,128)(2,1)S(1)}, bf16[224,1024]{1,0:T(8,128)(2,1)S(1)}, u32[]{:S(2)}, u32[]{:S(2)}) %collective-permute-start.40) | collective-permute-done | bytes 458784 | tf_op jit(solution)/shard_map/ppermute | solution.py:171
  284.8 10.3 %collective-permute-start.42 = (bf16[224,512]{1,0:T(8,128)(2,1)S(1)}, bf16[224,512]{1,0:T(8,128)(2,1)S(1)}, u32[]{:S(2)}, u32[]{:S(2)}) collective-permute-start(bf16[224,512]{1,0:T(8,128)(2,1)S(1)} %slice.264), channel_id=1, source_target_pairs={{0,6},{1,7},{2,0},{3,1},{4,2},{5,3},{6,4},{7,5},{8,14},{9,15},{10,... | collective-permute-start | bytes 688136 | tf_op jit(solution)/shard_map/ppermute | solution.py:171
  295.2 5.4 %collective-permute-done.42 = bf16[224,512]{1,0:T(8,128)(2,1)S(1)} collective-permute-done((bf16[224,512]{1,0:T(8,128)(2,1)S(1)}, bf16[224,512]{1,0:T(8,128)(2,1)S(1)}, u32[]{:S(2)}, u32[]{:S(2)}) %collective-permute-start.42) | collective-permute-done | bytes 229408 | tf_op jit(solution)/shard_map/ppermute | solution.py:171
  316.4 8.2 %collective-permute-done.59 = bf16[448,512]{1,0:T(8,128)(2,1)S(1)} collective-permute-done((bf16[448,512]{1,0:T(8,128)(2,1)S(1)}, bf16[448,512]{1,0:T(8,128)(2,1)S(1)}, u32[]{:S(2)}, u32[]{:S(2)}) %collective-permute-start.59) | collective-permute-done | bytes 458784 | tf_op jit(solution)/shard_map/ppermute | solution.py:37
  326.6 7.8 %collective-permute-done.49 = bf16[448,512]{1,0:T(8,128)(2,1)S(1)} collective-permute-done((bf16[448,512]{1,0:T(8,128)(2,1)S(1)}, bf16[448,512]{1,0:T(8,128)(2,1)S(1)}, u32[]{:S(2)}, u32[]{:S(2)}) %collective-permute-start.49) | collective-permute-done | bytes 458784 | tf_op jit(solution)/shard_map/ppermute | solution.py:37
  335.1 9.2 %collective-permute-done.44 = bf16[448,512]{1,0:T(8,128)(2,1)S(1)} collective-permute-done((bf16[448,512]{1,0:T(8,128)(2,1)S(1)}, bf16[448,512]{1,0:T(8,128)(2,1)S(1)}, u32[]{:S(2)}, u32[]{:S(2)}) %collective-permute-start.44) | collective-permute-done | bytes 458784 | tf_op jit(solution)/shard_map/ppermute | solution.py:37
  346.1 8.0 %collective-permute-done.54 = bf16[448,512]{1,0:T(8,128)(2,1)S(1)} collective-permute-done((bf16[448,512]{1,0:T(8,128)(2,1)S(1)}, bf16[448,512]{1,0:T(8,128)(2,1)S(1)}, u32[]{:S(2)}, u32[]{:S(2)}) %collective-permute-start.54) | collective-permute-done | bytes 458784 | tf_op jit(solution)/shard_map/ppermute | solution.py:37
  356.3 7.6 %collective-permute-done.61 = bf16[448,512]{1,0:T(8,128)(2,1)S(1)} collective-permute-done((bf16[448,512]{1,0:T(8,128)(2,1)S(1)}, bf16[448,512]{1,0:T(8,128)(2,1)S(1)}, u32[]{:S(2)}, u32[]{:S(2)}) %collective-permute-start.61) | collective-permute-done | bytes 458784 | tf_op jit(solution)/shard_map/ppermute | solution.py:52
  365.4 8.3 %collective-permute-done.51 = bf16[448,512]{1,0:T(8,128)(2,1)S(1)} collective-permute-done((bf16[448,512]{1,0:T(8,128)(2,1)S(1)}, bf16[448,512]{1,0:T(8,128)(2,1)S(1)}, u32[]{:S(2)}, u32[]{:S(2)}) %collective-permute-start.51) | collective-permute-done | bytes 458784 | tf_op jit(solution)/shard_map/ppermute | solution.py:52
  374.4 9.2 %collective-permute-done.46 = bf16[448,512]{1,0:T(8,128)(2,1)S(1)} collective-permute-done((bf16[448,512]{1,0:T(8,128)(2,1)S(1)}, bf16[448,512]{1,0:T(8,128)(2,1)S(1)}, u32[]{:S(2)}, u32[]{:S(2)}) %collective-permute-start.46) | collective-permute-done | bytes 458784 | tf_op jit(solution)/shard_map/ppermute | solution.py:52
  383.6 8.9 %collective-permute-done.56 = bf16[448,512]{1,0:T(8,128)(2,1)S(1)} collective-permute-done((bf16[448,512]{1,0:T(8,128)(2,1)S(1)}, bf16[448,512]{1,0:T(8,128)(2,1)S(1)}, u32[]{:S(2)}, u32[]{:S(2)}) %collective-permute-start.56) | collective-permute-done | bytes 458784 | tf_op jit(solution)/shard_map/ppermute | solution.py:52
  394.9 5.1 fusion.31
  400.0 5.0 fusion.25
  405.0 8.0 %add_convert_fusion = bf16[1792,1024]{1,0:T(8,128)(2,1)S(1)} fusion(f32[1792,1024]{1,0:T(8,128)} %fusion.25, f32[1792,1024]{1,0:T(8,128)} %fusion.31, f32[1792,1024]{1,0:T(8,128)S(1)} %fusion.28, bf16[1792,512]{1,0:T(8,128)(2,1)S(1)} %bitcast.373, bf16[2048,1024]{1,0:T(8,128)(2,1)S(1)} %copy-done.10), kind=kOutput, calls=%fused_computation.2 | convolution fusion | flops 1886388224 | bytes 28573696 | tf_op jit(solution)/shard_map/dot_general | solution.py:148
  417.6 3.9 collective-permute-start.70
  424.1 4.8 collective-permute-done.65
  430.7 3.0 collective-permute-done.68
  433.9 4.7 collective-permute-done.70
  440.6 8.0 %collective-permute-done.64 = bf16[224,1024]{1,0:T(8,128)(2,1)S(1)} collective-permute-done((bf16[224,1024]{1,0:T(8,128)(2,1)S(1)}, bf16[224,1024]{1,0:T(8,128)(2,1)S(1)}, u32[]{:S(2)}, u32[]{:S(2)}) %collective-permute-start.64) | collective-permute-done | bytes 458784 | tf_op jit(solution)/shard_map/ppermute | solution.py:171
  448.5 9.8 %collective-permute-done.66 = bf16[224,1024]{1,0:T(8,128)(2,1)S(1)} collective-permute-done((bf16[224,1024]{1,0:T(8,128)(2,1)S(1)}, bf16[224,1024]{1,0:T(8,128)(2,1)S(1)}, u32[]{:S(2)}, u32[]{:S(2)}) %collective-permute-start.66) | collective-permute-done | bytes 458784 | tf_op jit(solution)/shard_map/ppermute | solution.py:171
  460.1 8.1 %collective-permute-done.69 = bf16[224,1024]{1,0:T(8,128)(2,1)S(1)} collective-permute-done((bf16[224,1024]{1,0:T(8,128)(2,1)S(1)}, bf16[224,1024]{1,0:T(8,128)(2,1)S(1)}, u32[]{:S(2)}, u32[]{:S(2)}) %collective-permute-start.69) | collective-permute-done | bytes 458784 | tf_op jit(solution)/shard_map/ppermute | solution.py:171
  468.2 8.7 %collective-permute-done.71 = bf16[224,1024]{1,0:T(8,128)(2,1)S(1)} collective-permute-done((bf16[224,1024]{1,0:T(8,128)(2,1)S(1)}, bf16[224,1024]{1,0:T(8,128)(2,1)S(1)}, u32[]{:S(2)}, u32[]{:S(2)}) %collective-permute-start.71) | collective-permute-done | bytes 458784 | tf_op jit(solution)/shard_map/ppermute | solution.py:171
  477.4 4.2 collective-permute-done.72
  482.6 3.9 collective-permute-done.73
  499.8 2.5 dynamic_update_slice.217
  502.3 2.6 dynamic_update_slice.218
  506.6 2.5 dynamic_update_slice.219
  509.1 2.6 dynamic_update_slice.220
  511.7 2.6 dynamic_update_slice.221
  514.3 2.6 dynamic_update_slice.222
  516.9 2.6 dynamic_update_slice.223
  (310 shorter events, 140.2 us)
Async XLA Ops:
  12.0 8.9 %collective-permute-start.4 = (bf16[1,56,1024]{2,0,1:T(2,128)(2,1)S(1)}, bf16[1,56,1024]{2,0,1:T(2,128)(2,1)S(1)}, u32[]{:S(2)}, u32[]{:S(2)}) collective-permute-start(bf16[1,56,1024]{2,0,1:T(2,128)(2,1)S(1)} %get-tuple-element.55), channel_id=1, source_target_pairs={{0,16},{8,24},{16,0},{24,8},{1,17},{9,25},{17,1},{25,9},{2,18},{10... | collective-permute-start | bytes 344072 | tf_op jit(solution)/shard_map/ppermute | solution.py:250
  14.5 10.3 %collective-permute-start.5 = (bf16[1,56,1024]{2,0,1:T(2,128)(2,1)S(1)}, bf16[1,56,1024]{2,0,1:T(2,128)(2,1)S(1)}, u32[]{:S(2)}, u32[]{:S(2)}) collective-permute-start(bf16[1,56,1024]{2,0,1:T(2,128)(2,1)S(1)} %get-tuple-element.54), channel_id=1, source_target_pairs={{0,24},{8,0},{16,8},{24,16},{1,25},{9,1},{17,9},{25,17},{2,26},{10... | collective-permute-start | bytes 344072 | tf_op jit(solution)/shard_map/ppermute | solution.py:250
  26.5 14.5 %collective-permute-start.6 = (bf16[224,1024]{1,0:T(8,128)(2,1)S(1)}, bf16[224,1024]{1,0:T(8,128)(2,1)S(1)}, u32[]{:S(2)}, u32[]{:S(2)}) collective-permute-start(bf16[224,1024]{1,0:T(8,128)(2,1)S(1)} %bitcast.394), channel_id=1, source_target_pairs={{0,2},{1,3},{2,4},{3,5},{4,6},{5,7},{6,0},{7,1},{8,10},{9,11},{10,... | collective-permute-start | bytes 1376264 | tf_op jit(solution)/shard_map/ppermute | solution.py:171
  28.1 23.2 %collective-permute-start.7 = (bf16[224,1024]{1,0:T(8,128)(2,1)S(1)}, bf16[224,1024]{1,0:T(8,128)(2,1)S(1)}, u32[]{:S(2)}, u32[]{:S(2)}) collective-permute-start(bf16[224,1024]{1,0:T(8,128)(2,1)S(1)} %bitcast.395), channel_id=1, source_target_pairs={{0,6},{1,7},{2,0},{3,1},{4,2},{5,3},{6,4},{7,5},{8,14},{9,15},{10,... | collective-permute-start | bytes 1376264 | tf_op jit(solution)/shard_map/ppermute | solution.py:171
  30.4 22.1 %collective-permute-start.10 = (bf16[224,1024]{1,0:T(8,128)(2,1)S(1)}, bf16[224,1024]{1,0:T(8,128)(2,1)S(1)}, u32[]{:S(2)}, u32[]{:S(2)}) collective-permute-start(bf16[224,1024]{1,0:T(8,128)(2,1)S(1)} %bitcast.396), channel_id=1, source_target_pairs={{0,1},{1,0},{2,3},{3,2},{4,5},{5,4},{6,7},{7,6},{8,9},{9,8},{10,11... | collective-permute-start | bytes 1376264 | tf_op jit(solution)/shard_map/ppermute | solution.py:178
  41.0 15.5 %collective-permute-start.8 = (bf16[224,512]{1,0:T(8,128)(2,1)S(1)}, bf16[224,512]{1,0:T(8,128)(2,1)S(1)}, u32[]{:S(2)}, u32[]{:S(2)}) collective-permute-start(bf16[224,512]{1,0:T(8,128)(2,1)S(1)} %slice.235), channel_id=1, source_target_pairs={{0,2},{1,3},{2,4},{3,5},{4,6},{5,7},{6,0},{7,1},{8,10},{9,11},{10,... | collective-permute-start | bytes 688136 | tf_op jit(solution)/shard_map/ppermute | solution.py:171
  51.3 18.3 %collective-permute-start.9 = (bf16[224,512]{1,0:T(8,128)(2,1)S(1)}, bf16[224,512]{1,0:T(8,128)(2,1)S(1)}, u32[]{:S(2)}, u32[]{:S(2)}) collective-permute-start(bf16[224,512]{1,0:T(8,128)(2,1)S(1)} %slice.236), channel_id=1, source_target_pairs={{0,6},{1,7},{2,0},{3,1},{4,2},{5,3},{6,4},{7,5},{8,14},{9,15},{10,... | collective-permute-start | bytes 688136 | tf_op jit(solution)/shard_map/ppermute | solution.py:171
  52.5 17.3 %collective-permute-start.11 = (bf16[224,1024]{1,0:T(8,128)(2,1)S(1)}, bf16[224,1024]{1,0:T(8,128)(2,1)S(1)}, u32[]{:S(2)}, u32[]{:S(2)}) collective-permute-start(bf16[224,1024]{1,0:T(8,128)(2,1)S(1)} %collective-permute-done.10), channel_id=1, source_target_pairs={{0,2},{1,3},{2,4},{3,5},{4,6},{5,7},{6,0},{7,1},{8,10},{9,11},{10,... | collective-permute-start | bytes 1376264 | tf_op jit(solution)/shard_map/ppermute | solution.py:171
  53.4 30.3 %collective-permute-start.12 = (bf16[224,1024]{1,0:T(8,128)(2,1)S(1)}, bf16[224,1024]{1,0:T(8,128)(2,1)S(1)}, u32[]{:S(2)}, u32[]{:S(2)}) collective-permute-start(bf16[224,1024]{1,0:T(8,128)(2,1)S(1)} %collective-permute-done.10), channel_id=1, source_target_pairs={{0,6},{1,7},{2,0},{3,1},{4,2},{5,3},{6,4},{7,5},{8,14},{9,15},{10,... | collective-permute-start | bytes 1376264 | tf_op jit(solution)/shard_map/ppermute | solution.py:171
  69.8 14.2 %collective-permute-start.13 = (bf16[224,512]{1,0:T(8,128)(2,1)S(1)}, bf16[224,512]{1,0:T(8,128)(2,1)S(1)}, u32[]{:S(2)}, u32[]{:S(2)}) collective-permute-start(bf16[224,512]{1,0:T(8,128)(2,1)S(1)} %slice.237), channel_id=1, source_target_pairs={{0,2},{1,3},{2,4},{3,5},{4,6},{5,7},{6,0},{7,1},{8,10},{9,11},{10,... | collective-permute-start | bytes 688136 | tf_op jit(solution)/shard_map/ppermute | solution.py:171
  104.1 103.6 %collective-permute-start = (bf16[1,56,1024]{2,1,0:T(8,128)(2,1)}, bf16[1,56,1024]{2,1,0:T(8,128)(2,1)S(1)}, u32[]{:S(2)}, u32[]{:S(2)}) collective-permute-start(bf16[1,56,1024]{2,1,0:T(8,128)(2,1)} %bitcast.365), channel_id=1, source_target_pairs={{0,8},{8,16},{16,24},{24,0},{1,9},{9,17},{17,25},{25,1},{2,10},{10... | collective-permute-start | bytes 344072 | tf_op jit(solution)/shard_map/ppermute | solution.py:250
  107.2 17.8 %collective-permute-start.16 = (bf16[224,1536]{1,0:T(8,128)(2,1)S(1)}, bf16[224,1536]{1,0:T(8,128)(2,1)S(1)}, u32[]{:S(2)}, u32[]{:S(2)}) collective-permute-start(bf16[224,1536]{1,0:T(8,128)(2,1)S(1)} %dynamic-slice_bitcast_fusion.7), channel_id=1, source_target_pairs={{0,16},{8,24},{16,0},{24,8},{1,17},{9,25},{17,1},{25,9},{2,18},{10... | collective-permute-start | bytes 2064392 | tf_op jit(solution)/shard_map/ppermute | solution.py:37
  111.7 28.2 %collective-permute-start.21 = (bf16[224,1536]{1,0:T(8,128)(2,1)}, bf16[224,1536]{1,0:T(8,128)(2,1)}, u32[]{:S(2)}, u32[]{:S(2)}) collective-permute-start(bf16[224,1536]{1,0:T(8,128)(2,1)} %dynamic-slice_bitcast_fusion.6), channel_id=1, source_target_pairs={{0,16},{8,24},{16,0},{24,8},{1,17},{9,25},{17,1},{25,9},{2,18},{10... | collective-permute-start | bytes 2064392 | tf_op jit(solution)/shard_map/ppermute | solution.py:37
  134.7 19.3 %collective-permute-start.17 = (bf16[224,512]{1,0:T(8,128)(2,1)}, bf16[224,512]{1,0:T(8,128)(2,1)}, u32[]{:S(2)}, u32[]{:S(2)}) collective-permute-start(bf16[224,512]{1,0:T(8,128)(2,1)} %bitcast.362), channel_id=1, source_target_pairs={{0,8},{8,0},{16,24},{24,16},{1,9},{9,1},{17,25},{25,17},{2,10},{10... | collective-permute-start | bytes 688136 | tf_op jit(solution)/shard_map/ppermute | solution.py:53
  136.0 11.9 %collective-permute-start.18 = (bf16[224,512]{1,0:T(8,128)(2,1)}, bf16[224,512]{1,0:T(8,128)(2,1)}, u32[]{:S(2)}, u32[]{:S(2)}) collective-permute-start(bf16[224,512]{1,0:T(8,128)(2,1)} %bitcast.362), channel_id=1, source_target_pairs={{0,16},{8,24},{16,0},{24,8},{1,17},{9,25},{17,1},{25,9},{2,18},{10... | collective-permute-start | bytes 688136 | tf_op jit(solution)/shard_map/ppermute | solution.py:52
  145.1 10.7 %collective-permute-start.22 = (bf16[224,512]{1,0:T(8,128)(2,1)S(1)}, bf16[224,512]{1,0:T(8,128)(2,1)S(1)}, u32[]{:S(2)}, u32[]{:S(2)}) collective-permute-start(bf16[224,512]{1,0:T(8,128)(2,1)S(1)} %bitcast.415), channel_id=1, source_target_pairs={{0,8},{8,0},{16,24},{24,16},{1,9},{9,1},{17,25},{25,17},{2,10},{10... | collective-permute-start | bytes 688136 | tf_op jit(solution)/shard_map/ppermute | solution.py:53
  159.0 10.4 %collective-permute-start.25 = (bf16[224,512]{1,0:T(8,128)(2,1)S(1)}, bf16[224,512]{1,0:T(8,128)(2,1)S(1)}, u32[]{:S(2)}, u32[]{:S(2)}) collective-permute-start(bf16[224,512]{1,0:T(8,128)(2,1)S(1)} %get-tuple-element.50), channel_id=1, source_target_pairs={{0,2},{1,3},{2,4},{3,5},{4,6},{5,7},{6,0},{7,1},{8,10},{9,11},{10,... | collective-permute-start | bytes 688136 | tf_op jit(solution)/shard_map/ppermute | solution.py:171
  160.9 13.5 %collective-permute-start.27 = (bf16[224,512]{1,0:T(8,128)(2,1)S(1)}, bf16[224,512]{1,0:T(8,128)(2,1)S(1)}, u32[]{:S(2)}, u32[]{:S(2)}) collective-permute-start(bf16[224,512]{1,0:T(8,128)(2,1)S(1)} %get-tuple-element.51), channel_id=1, source_target_pairs={{0,6},{1,7},{2,0},{3,1},{4,2},{5,3},{6,4},{7,5},{8,14},{9,15},{10,... | collective-permute-start | bytes 688136 | tf_op jit(solution)/shard_map/ppermute | solution.py:171
  163.1 16.2 %collective-permute-start.30 = (bf16[224,512]{1,0:T(8,128)(2,1)S(1)}, bf16[224,512]{1,0:T(8,128)(2,1)S(1)}, u32[]{:S(2)}, u32[]{:S(2)}) collective-permute-start(bf16[224,512]{1,0:T(8,128)(2,1)S(1)} %get-tuple-element.52), channel_id=1, source_target_pairs={{0,2},{1,3},{2,4},{3,5},{4,6},{5,7},{6,0},{7,1},{8,10},{9,11},{10,... | collective-permute-start | bytes 688136 | tf_op jit(solution)/shard_map/ppermute | solution.py:171
  163.1 21.1 %collective-permute-start.32 = (bf16[224,512]{1,0:T(8,128)(2,1)S(1)}, bf16[224,512]{1,0:T(8,128)(2,1)S(1)}, u32[]{:S(2)}, u32[]{:S(2)}) collective-permute-start(bf16[224,512]{1,0:T(8,128)(2,1)S(1)} %get-tuple-element.53), channel_id=1, source_target_pairs={{0,6},{1,7},{2,0},{3,1},{4,2},{5,3},{6,4},{7,5},{8,14},{9,15},{10,... | collective-permute-start | bytes 688136 | tf_op jit(solution)/shard_map/ppermute | solution.py:171
  169.6 24.5 %collective-permute-start.26 = (bf16[224,1024]{1,0:T(8,128)(2,1)S(1)}, bf16[224,1024]{1,0:T(8,128)(2,1)S(1)}, u32[]{:S(2)}, u32[]{:S(2)}) collective-permute-start(bf16[224,1024]{1,0:T(8,128)(2,1)S(1)} %pad_maximum_fusion.1), channel_id=1, source_target_pairs={{0,2},{1,3},{2,4},{3,5},{4,6},{5,7},{6,0},{7,1},{8,10},{9,11},{10,... | collective-permute-start | bytes 1376264 | tf_op jit(solution)/shard_map/ppermute | solution.py:171
  174.5 29.3 %collective-permute-start.28 = (bf16[224,1024]{1,0:T(8,128)(2,1)S(1)}, bf16[224,1024]{1,0:T(8,128)(2,1)S(1)}, u32[]{:S(2)}, u32[]{:S(2)}) collective-permute-start(bf16[224,1024]{1,0:T(8,128)(2,1)S(1)} %pad_maximum_fusion.2), channel_id=1, source_target_pairs={{0,6},{1,7},{2,0},{3,1},{4,2},{5,3},{6,4},{7,5},{8,14},{9,15},{10,... | collective-permute-start | bytes 1376264 | tf_op jit(solution)/shard_map/ppermute | solution.py:171
  180.2 33.5 %collective-permute-start.31 = (bf16[224,1024]{1,0:T(8,128)(2,1)}, bf16[224,1024]{1,0:T(8,128)(2,1)S(1)}, u32[]{:S(2)}, u32[]{:S(2)}) collective-permute-start(bf16[224,1024]{1,0:T(8,128)(2,1)} %pad_maximum_fusion.3), channel_id=1, source_target_pairs={{0,2},{1,3},{2,4},{3,5},{4,6},{5,7},{6,0},{7,1},{8,10},{9,11},{10,... | collective-permute-start | bytes 1376264 | tf_op jit(solution)/shard_map/ppermute | solution.py:171
  185.1 37.6 %collective-permute-start.33 = (bf16[224,1024]{1,0:T(8,128)(2,1)}, bf16[224,1024]{1,0:T(8,128)(2,1)S(1)}, u32[]{:S(2)}, u32[]{:S(2)}) collective-permute-start(bf16[224,1024]{1,0:T(8,128)(2,1)} %pad_maximum_fusion.4), channel_id=1, source_target_pairs={{0,6},{1,7},{2,0},{3,1},{4,2},{5,3},{6,4},{7,5},{8,14},{9,15},{10,... | collective-permute-start | bytes 1376264 | tf_op jit(solution)/shard_map/ppermute | solution.py:171
  204.1 18.7 %collective-permute-start.29 = (bf16[224,1024]{1,0:T(8,128)(2,1)S(1)}, bf16[224,1024]{1,0:T(8,128)(2,1)S(1)}, u32[]{:S(2)}, u32[]{:S(2)}) collective-permute-start(bf16[224,1024]{1,0:T(8,128)(2,1)S(1)} %fusion.88), channel_id=1, source_target_pairs={{0,1},{1,0},{2,3},{3,2},{4,5},{5,4},{6,7},{7,6},{8,9},{9,8},{10,11... | collective-permute-start | bytes 1376264 | tf_op jit(solution)/shard_map/ppermute | solution.py:178
  230.8 15.3 %collective-permute-start.34 = (bf16[224,1024]{1,0:T(8,128)(2,1)S(1)}, bf16[224,1024]{1,0:T(8,128)(2,1)S(1)}, u32[]{:S(2)}, u32[]{:S(2)}) collective-permute-start(bf16[224,1024]{1,0:T(8,128)(2,1)S(1)} %get-tuple-element.16), channel_id=1, source_target_pairs={{0,2},{1,3},{2,4},{3,5},{4,6},{5,7},{6,0},{7,1},{8,10},{9,11},{10,... | collective-permute-start | bytes 1376264 | tf_op jit(solution)/shard_map/ppermute | solution.py:171
  231.1 22.4 %collective-permute-start.35 = (bf16[224,1024]{1,0:T(8,128)(2,1)S(1)}, bf16[224,1024]{1,0:T(8,128)(2,1)S(1)}, u32[]{:S(2)}, u32[]{:S(2)}) collective-permute-start(bf16[224,1024]{1,0:T(8,128)(2,1)S(1)} %get-tuple-element.16), channel_id=1, source_target_pairs={{0,6},{1,7},{2,0},{3,1},{4,2},{5,3},{6,4},{7,5},{8,14},{9,15},{10,... | collective-permute-start | bytes 1376264 | tf_op jit(solution)/shard_map/ppermute | solution.py:171
  234.6 21.6 %collective-permute-start.38 = (bf16[224,1024]{1,0:T(8,128)(2,1)S(1)}, bf16[224,1024]{1,0:T(8,128)(2,1)S(1)}, u32[]{:S(2)}, u32[]{:S(2)}) collective-permute-start(bf16[224,1024]{1,0:T(8,128)(2,1)S(1)} %get-tuple-element.16), channel_id=1, source_target_pairs={{0,1},{1,0},{2,3},{3,2},{4,5},{5,4},{6,7},{7,6},{8,9},{9,8},{10,11... | collective-permute-start | bytes 1376264 | tf_op jit(solution)/shard_map/ppermute | solution.py:178
  246.1 14.8 %collective-permute-start.36 = (bf16[224,512]{1,0:T(8,128)(2,1)S(1)}, bf16[224,512]{1,0:T(8,128)(2,1)S(1)}, u32[]{:S(2)}, u32[]{:S(2)}) collective-permute-start(bf16[224,512]{1,0:T(8,128)(2,1)S(1)} %slice.261), channel_id=1, source_target_pairs={{0,2},{1,3},{2,4},{3,5},{4,6},{5,7},{6,0},{7,1},{8,10},{9,11},{10,... | collective-permute-start | bytes 688136 | tf_op jit(solution)/shard_map/ppermute | solution.py:171
  253.5 12.3 %collective-permute-start.37 = (bf16[224,512]{1,0:T(8,128)(2,1)S(1)}, bf16[224,512]{1,0:T(8,128)(2,1)S(1)}, u32[]{:S(2)}, u32[]{:S(2)}) collective-permute-start(bf16[224,512]{1,0:T(8,128)(2,1)S(1)} %slice.262), channel_id=1, source_target_pairs={{0,6},{1,7},{2,0},{3,1},{4,2},{5,3},{6,4},{7,5},{8,14},{9,15},{10,... | collective-permute-start | bytes 688136 | tf_op jit(solution)/shard_map/ppermute | solution.py:171
  256.3 19.4 %collective-permute-start.39 = (bf16[224,1024]{1,0:T(8,128)(2,1)S(1)}, bf16[224,1024]{1,0:T(8,128)(2,1)S(1)}, u32[]{:S(2)}, u32[]{:S(2)}) collective-permute-start(bf16[224,1024]{1,0:T(8,128)(2,1)S(1)} %collective-permute-done.38), channel_id=1, source_target_pairs={{0,2},{1,3},{2,4},{3,5},{4,6},{5,7},{6,0},{7,1},{8,10},{9,11},{10,... | collective-permute-start | bytes 1376264 | tf_op jit(solution)/shard_map/ppermute | solution.py:171
  256.3 28.5 %collective-permute-start.40 = (bf16[224,1024]{1,0:T(8,128)(2,1)S(1)}, bf16[224,1024]{1,0:T(8,128)(2,1)S(1)}, u32[]{:S(2)}, u32[]{:S(2)}) collective-permute-start(bf16[224,1024]{1,0:T(8,128)(2,1)S(1)} %collective-permute-done.38), channel_id=1, source_target_pairs={{0,6},{1,7},{2,0},{3,1},{4,2},{5,3},{6,4},{7,5},{8,14},{9,15},{10,... | collective-permute-start | bytes 1376264 | tf_op jit(solution)/shard_map/ppermute | solution.py:171
  275.6 19.6 %collective-permute-start.41 = (bf16[224,512]{1,0:T(8,128)(2,1)S(1)}, bf16[224,512]{1,0:T(8,128)(2,1)S(1)}, u32[]{:S(2)}, u32[]{:S(2)}) collective-permute-start(bf16[224,512]{1,0:T(8,128)(2,1)S(1)} %slice.263), channel_id=1, source_target_pairs={{0,2},{1,3},{2,4},{3,5},{4,6},{5,7},{6,0},{7,1},{8,10},{9,11},{10,... | collective-permute-start | bytes 688136 | tf_op jit(solution)/shard_map/ppermute | solution.py:171
  284.8 15.8 %collective-permute-start.42 = (bf16[224,512]{1,0:T(8,128)(2,1)S(1)}, bf16[224,512]{1,0:T(8,128)(2,1)S(1)}, u32[]{:S(2)}, u32[]{:S(2)}) collective-permute-start(bf16[224,512]{1,0:T(8,128)(2,1)S(1)} %slice.264), channel_id=1, source_target_pairs={{0,6},{1,7},{2,0},{3,1},{4,2},{5,3},{6,4},{7,5},{8,14},{9,15},{10,... | collective-permute-start | bytes 688136 | tf_op jit(solution)/shard_map/ppermute | solution.py:171
  311.2 13.5 %collective-permute-start.59 = (bf16[448,512]{1,0:T(8,128)(2,1)S(1)}, bf16[448,512]{1,0:T(8,128)(2,1)S(1)}, u32[]{:S(2)}, u32[]{:S(2)}) collective-permute-start(bf16[448,512]{1,0:T(8,128)(2,1)S(1)} %dynamic-slice_bitcast_fusion.14), channel_id=1, source_target_pairs={{0,16},{8,24},{16,0},{24,8},{1,17},{9,25},{17,1},{25,9},{2,18},{10... | collective-permute-start | bytes 1376264 | tf_op jit(solution)/shard_map/ppermute | solution.py:37
  312.9 21.6 %collective-permute-start.49 = (bf16[448,512]{1,0:T(8,128)(2,1)S(1)}, bf16[448,512]{1,0:T(8,128)(2,1)S(1)}, u32[]{:S(2)}, u32[]{:S(2)}) collective-permute-start(bf16[448,512]{1,0:T(8,128)(2,1)S(1)} %dynamic-slice_bitcast_fusion.16), channel_id=1, source_target_pairs={{0,16},{8,24},{16,0},{24,8},{1,17},{9,25},{17,1},{25,9},{2,18},{10... | collective-permute-start | bytes 1376264 | tf_op jit(solution)/shard_map/ppermute | solution.py:37
  313.9 30.3 %collective-permute-start.44 = (bf16[448,512]{1,0:T(8,128)(2,1)S(1)}, bf16[448,512]{1,0:T(8,128)(2,1)S(1)}, u32[]{:S(2)}, u32[]{:S(2)}) collective-permute-start(bf16[448,512]{1,0:T(8,128)(2,1)S(1)} %dynamic-slice_bitcast_fusion.17), channel_id=1, source_target_pairs={{0,16},{8,24},{16,0},{24,8},{1,17},{9,25},{17,1},{25,9},{2,18},{10... | collective-permute-start | bytes 1376264 | tf_op jit(solution)/shard_map/ppermute | solution.py:37
  315.7 38.4 %collective-permute-start.54 = (bf16[448,512]{1,0:T(8,128)(2,1)S(1)}, bf16[448,512]{1,0:T(8,128)(2,1)S(1)}, u32[]{:S(2)}, u32[]{:S(2)}) collective-permute-start(bf16[448,512]{1,0:T(8,128)(2,1)S(1)} %dynamic-slice_bitcast_fusion.15), channel_id=1, source_target_pairs={{0,16},{8,24},{16,0},{24,8},{1,17},{9,25},{17,1},{25,9},{2,18},{10... | collective-permute-start | bytes 1376264 | tf_op jit(solution)/shard_map/ppermute | solution.py:37
  325.2 29.7 %collective-permute-start.60 = (bf16[448,512]{1,0:T(8,128)(2,1)S(1)}, bf16[448,512]{1,0:T(8,128)(2,1)S(1)}, u32[]{:S(2)}, u32[]{:S(2)}) collective-permute-start(bf16[448,512]{1,0:T(8,128)(2,1)S(1)} %get-tuple-element.8), channel_id=1, source_target_pairs={{0,8},{8,0},{16,24},{24,16},{1,9},{9,1},{17,25},{25,17},{2,10},{10... | collective-permute-start | bytes 1376264 | tf_op jit(solution)/shard_map/ppermute | solution.py:53
  325.2 38.7 %collective-permute-start.61 = (bf16[448,512]{1,0:T(8,128)(2,1)S(1)}, bf16[448,512]{1,0:T(8,128)(2,1)S(1)}, u32[]{:S(2)}, u32[]{:S(2)}) collective-permute-start(bf16[448,512]{1,0:T(8,128)(2,1)S(1)} %get-tuple-element.8), channel_id=1, source_target_pairs={{0,16},{8,24},{16,0},{24,8},{1,17},{9,25},{17,1},{25,9},{2,18},{10... | collective-permute-start | bytes 1376264 | tf_op jit(solution)/shard_map/ppermute | solution.py:52
  335.0 29.0 %collective-permute-start.50 = (bf16[448,512]{1,0:T(8,128)(2,1)S(1)}, bf16[448,512]{1,0:T(8,128)(2,1)S(1)}, u32[]{:S(2)}, u32[]{:S(2)}) collective-permute-start(bf16[448,512]{1,0:T(8,128)(2,1)S(1)} %get-tuple-element.10), channel_id=1, source_target_pairs={{0,8},{8,0},{16,24},{24,16},{1,9},{9,1},{17,25},{25,17},{2,10},{10... | collective-permute-start | bytes 1376264 | tf_op jit(solution)/shard_map/ppermute | solution.py:53
  344.3 29.5 %collective-permute-start.51 = (bf16[448,512]{1,0:T(8,128)(2,1)S(1)}, bf16[448,512]{1,0:T(8,128)(2,1)S(1)}, u32[]{:S(2)}, u32[]{:S(2)}) collective-permute-start(bf16[448,512]{1,0:T(8,128)(2,1)S(1)} %get-tuple-element.10), channel_id=1, source_target_pairs={{0,16},{8,24},{16,0},{24,8},{1,17},{9,25},{17,1},{25,9},{2,18},{10... | collective-permute-start | bytes 1376264 | tf_op jit(solution)/shard_map/ppermute | solution.py:52
  354.1 19.7 %collective-permute-start.45 = (bf16[448,512]{1,0:T(8,128)(2,1)S(1)}, bf16[448,512]{1,0:T(8,128)(2,1)S(1)}, u32[]{:S(2)}, u32[]{:S(2)}) collective-permute-start(bf16[448,512]{1,0:T(8,128)(2,1)S(1)} %get-tuple-element.12), channel_id=1, source_target_pairs={{0,8},{8,0},{16,24},{24,16},{1,9},{9,1},{17,25},{25,17},{2,10},{10... | collective-permute-start | bytes 1376264 | tf_op jit(solution)/shard_map/ppermute | solution.py:53
  354.9 28.7 %collective-permute-start.46 = (bf16[448,512]{1,0:T(8,128)(2,1)S(1)}, bf16[448,512]{1,0:T(8,128)(2,1)S(1)}, u32[]{:S(2)}, u32[]{:S(2)}) collective-permute-start(bf16[448,512]{1,0:T(8,128)(2,1)S(1)} %get-tuple-element.12), channel_id=1, source_target_pairs={{0,16},{8,24},{16,0},{24,8},{1,17},{9,25},{17,1},{25,9},{2,18},{10... | collective-permute-start | bytes 1376264 | tf_op jit(solution)/shard_map/ppermute | solution.py:52
  363.9 28.6 %collective-permute-start.55 = (bf16[448,512]{1,0:T(8,128)(2,1)S(1)}, bf16[448,512]{1,0:T(8,128)(2,1)S(1)}, u32[]{:S(2)}, u32[]{:S(2)}) collective-permute-start(bf16[448,512]{1,0:T(8,128)(2,1)S(1)} %get-tuple-element.14), channel_id=1, source_target_pairs={{0,8},{8,0},{16,24},{24,16},{1,9},{9,1},{17,25},{25,17},{2,10},{10... | collective-permute-start | bytes 1376264 | tf_op jit(solution)/shard_map/ppermute | solution.py:53
  364.0 28.5 %collective-permute-start.56 = (bf16[448,512]{1,0:T(8,128)(2,1)S(1)}, bf16[448,512]{1,0:T(8,128)(2,1)S(1)}, u32[]{:S(2)}, u32[]{:S(2)}) collective-permute-start(bf16[448,512]{1,0:T(8,128)(2,1)S(1)} %get-tuple-element.14), channel_id=1, source_target_pairs={{0,16},{8,24},{16,0},{24,8},{1,17},{9,25},{17,1},{25,9},{2,18},{10... | collective-permute-start | bytes 1376264 | tf_op jit(solution)/shard_map/ppermute | solution.py:52
  373.8 31.2 %collective-permute-start.62 = (bf16[448,512]{1,0:T(8,128)(2,1)S(1)}, bf16[448,512]{1,0:T(8,128)(2,1)S(1)}, u32[]{:S(2)}, u32[]{:S(2)}) collective-permute-start(bf16[448,512]{1,0:T(8,128)(2,1)S(1)} %collective-permute-done.61), channel_id=1, source_target_pairs={{0,8},{8,0},{16,24},{24,16},{1,9},{9,1},{17,25},{25,17},{2,10},{10... | collective-permute-start | bytes 1376264 | tf_op jit(solution)/shard_map/ppermute | solution.py:53
  373.8 18.9 %collective-permute-start.52 = (bf16[448,512]{1,0:T(8,128)(2,1)S(1)}, bf16[448,512]{1,0:T(8,128)(2,1)S(1)}, u32[]{:S(2)}, u32[]{:S(2)}) collective-permute-start(bf16[448,512]{1,0:T(8,128)(2,1)S(1)} %collective-permute-done.51), channel_id=1, source_target_pairs={{0,8},{8,0},{16,24},{24,16},{1,9},{9,1},{17,25},{25,17},{2,10},{10... | collective-permute-start | bytes 1376264 | tf_op jit(solution)/shard_map/ppermute | solution.py:53
  383.6 11.2 %collective-permute-start.47 = (bf16[448,512]{1,0:T(8,128)(2,1)S(1)}, bf16[448,512]{1,0:T(8,128)(2,1)S(1)}, u32[]{:S(2)}, u32[]{:S(2)}) collective-permute-start(bf16[448,512]{1,0:T(8,128)(2,1)S(1)} %collective-permute-done.46), channel_id=1, source_target_pairs={{0,8},{8,0},{16,24},{24,16},{1,9},{9,1},{17,25},{25,17},{2,10},{10... | collective-permute-start | bytes 1376264 | tf_op jit(solution)/shard_map/ppermute | solution.py:53
  413.5 10.4 %collective-permute-start.63 = (bf16[224,512]{1,0:T(8,128)(2,1)S(1)}, bf16[224,512]{1,0:T(8,128)(2,1)S(1)}, u32[]{:S(2)}, u32[]{:S(2)}) collective-permute-start(bf16[224,512]{1,0:T(8,128)(2,1)S(1)} %get-tuple-element.43), channel_id=1, source_target_pairs={{0,2},{1,3},{2,4},{3,5},{4,6},{5,7},{6,0},{7,1},{8,10},{9,11},{10,... | collective-permute-start | bytes 688136 | tf_op jit(solution)/shard_map/ppermute | solution.py:171
  415.1 13.8 %collective-permute-start.65 = (bf16[224,512]{1,0:T(8,128)(2,1)S(1)}, bf16[224,512]{1,0:T(8,128)(2,1)S(1)}, u32[]{:S(2)}, u32[]{:S(2)}) collective-permute-start(bf16[224,512]{1,0:T(8,128)(2,1)S(1)} %get-tuple-element.44), channel_id=1, source_target_pairs={{0,6},{1,7},{2,0},{3,1},{4,2},{5,3},{6,4},{7,5},{8,14},{9,15},{10,... | collective-permute-start | bytes 688136 | tf_op jit(solution)/shard_map/ppermute | solution.py:171
  417.5 16.2 %collective-permute-start.68 = (bf16[224,512]{1,0:T(8,128)(2,1)S(1)}, bf16[224,512]{1,0:T(8,128)(2,1)S(1)}, u32[]{:S(2)}, u32[]{:S(2)}) collective-permute-start(bf16[224,512]{1,0:T(8,128)(2,1)S(1)} %get-tuple-element.45), channel_id=1, source_target_pairs={{0,2},{1,3},{2,4},{3,5},{4,6},{5,7},{6,0},{7,1},{8,10},{9,11},{10,... | collective-permute-start | bytes 688136 | tf_op jit(solution)/shard_map/ppermute | solution.py:171
  417.6 21.1 %collective-permute-start.70 = (bf16[224,512]{1,0:T(8,128)(2,1)S(1)}, bf16[224,512]{1,0:T(8,128)(2,1)S(1)}, u32[]{:S(2)}, u32[]{:S(2)}) collective-permute-start(bf16[224,512]{1,0:T(8,128)(2,1)S(1)} %get-tuple-element.46), channel_id=1, source_target_pairs={{0,6},{1,7},{2,0},{3,1},{4,2},{5,3},{6,4},{7,5},{8,14},{9,15},{10,... | collective-permute-start | bytes 688136 | tf_op jit(solution)/shard_map/ppermute | solution.py:171
  424.0 24.5 %collective-permute-start.64 = (bf16[224,1024]{1,0:T(8,128)(2,1)S(1)}, bf16[224,1024]{1,0:T(8,128)(2,1)S(1)}, u32[]{:S(2)}, u32[]{:S(2)}) collective-permute-start(bf16[224,1024]{1,0:T(8,128)(2,1)S(1)} %pad_maximum_fusion.5), channel_id=1, source_target_pairs={{0,2},{1,3},{2,4},{3,5},{4,6},{5,7},{6,0},{7,1},{8,10},{9,11},{10,... | collective-permute-start | bytes 1376264 | tf_op jit(solution)/shard_map/ppermute | solution.py:171
  429.0 29.3 %collective-permute-start.66 = (bf16[224,1024]{1,0:T(8,128)(2,1)S(1)}, bf16[224,1024]{1,0:T(8,128)(2,1)S(1)}, u32[]{:S(2)}, u32[]{:S(2)}) collective-permute-start(bf16[224,1024]{1,0:T(8,128)(2,1)S(1)} %pad_maximum_fusion.6), channel_id=1, source_target_pairs={{0,6},{1,7},{2,0},{3,1},{4,2},{5,3},{6,4},{7,5},{8,14},{9,15},{10,... | collective-permute-start | bytes 1376264 | tf_op jit(solution)/shard_map/ppermute | solution.py:171
  433.9 34.4 %collective-permute-start.69 = (bf16[224,1024]{1,0:T(8,128)(2,1)S(1)}, bf16[224,1024]{1,0:T(8,128)(2,1)S(1)}, u32[]{:S(2)}, u32[]{:S(2)}) collective-permute-start(bf16[224,1024]{1,0:T(8,128)(2,1)S(1)} %pad_maximum_fusion.7), channel_id=1, source_target_pairs={{0,2},{1,3},{2,4},{3,5},{4,6},{5,7},{6,0},{7,1},{8,10},{9,11},{10,... | collective-permute-start | bytes 1376264 | tf_op jit(solution)/shard_map/ppermute | solution.py:171
  438.8 38.1 %collective-permute-start.71 = (bf16[224,1024]{1,0:T(8,128)(2,1)S(1)}, bf16[224,1024]{1,0:T(8,128)(2,1)S(1)}, u32[]{:S(2)}, u32[]{:S(2)}) collective-permute-start(bf16[224,1024]{1,0:T(8,128)(2,1)S(1)} %pad_maximum_fusion.8), channel_id=1, source_target_pairs={{0,6},{1,7},{2,0},{3,1},{4,2},{5,3},{6,4},{7,5},{8,14},{9,15},{10,... | collective-permute-start | bytes 1376264 | tf_op jit(solution)/shard_map/ppermute | solution.py:171
  458.5 18.4 %collective-permute-start.67 = (bf16[224,1024]{1,0:T(8,128)(2,1)S(1)}, bf16[224,1024]{1,0:T(8,128)(2,1)S(1)}, u32[]{:S(2)}, u32[]{:S(2)}) collective-permute-start(bf16[224,1024]{1,0:T(8,128)(2,1)S(1)} %fusion.81), channel_id=1, source_target_pairs={{0,1},{1,0},{2,3},{3,2},{4,5},{5,4},{6,7},{7,6},{8,9},{9,8},{10,11... | collective-permute-start | bytes 1376264 | tf_op jit(solution)/shard_map/ppermute | solution.py:178
  487.9 8.8 %collective-permute-start.75 = (bf16[1,56,512]{2,0,1:T(2,128)(2,1)S(1)}, bf16[1,56,512]{2,0,1:T(2,128)(2,1)S(1)}, u32[]{:S(2)}, u32[]{:S(2)}) collective-permute-start(bf16[1,56,512]{2,0,1:T(2,128)(2,1)S(1)} %get-tuple-element.39), channel_id=1, source_target_pairs={{0,1},{1,2},{2,3},{3,4},{4,5},{5,6},{6,7},{7,0},{8,9},{9,10},{10,1... | collective-permute-start | bytes 172040 | tf_op jit(solution)/shard_map/ppermute | solution.py:250
  490.8 15.8 %collective-permute-start.77 = (bf16[1,56,512]{2,0,1:T(2,128)(2,1)S(1)}, bf16[1,56,512]{2,0,1:T(2,128)(2,1)S(1)}, u32[]{:S(2)}, u32[]{:S(2)}) collective-permute-start(bf16[1,56,512]{2,0,1:T(2,128)(2,1)S(1)} %get-tuple-element.37), channel_id=1, source_target_pairs={{0,3},{1,4},{2,5},{3,6},{4,7},{5,0},{6,1},{7,2},{8,11},{9,12},{10,... | collective-permute-start | bytes 172040 | tf_op jit(solution)/shard_map/ppermute | solution.py:250
  492.6 16.5 %collective-permute-start.78 = (bf16[1,56,512]{2,0,1:T(2,128)(2,1)S(1)}, bf16[1,56,512]{2,0,1:T(2,128)(2,1)S(1)}, u32[]{:S(2)}, u32[]{:S(2)}) collective-permute-start(bf16[1,56,512]{2,0,1:T(2,128)(2,1)S(1)} %get-tuple-element.36), channel_id=1, source_target_pairs={{0,4},{1,5},{2,6},{3,7},{4,0},{5,1},{6,2},{7,3},{8,12},{9,13},{10,... | collective-permute-start | bytes 172040 | tf_op jit(solution)/shard_map/ppermute | solution.py:250
  494.6 17.1 %collective-permute-start.79 = (bf16[1,56,512]{2,0,1:T(2,128)(2,1)S(1)}, bf16[1,56,512]{2,0,1:T(2,128)(2,1)S(1)}, u32[]{:S(2)}, u32[]{:S(2)}) collective-permute-start(bf16[1,56,512]{2,0,1:T(2,128)(2,1)S(1)} %get-tuple-element.35), channel_id=1, source_target_pairs={{0,5},{1,6},{2,7},{3,0},{4,1},{5,2},{6,3},{7,4},{8,13},{9,14},{10,... | collective-permute-start | bytes 172040 | tf_op jit(solution)/shard_map/ppermute | solution.py:250
  496.7 17.5 %collective-permute-start.80 = (bf16[1,56,512]{2,0,1:T(2,128)(2,1)S(1)}, bf16[1,56,512]{2,0,1:T(2,128)(2,1)S(1)}, u32[]{:S(2)}, u32[]{:S(2)}) collective-permute-start(bf16[1,56,512]{2,0,1:T(2,128)(2,1)S(1)} %get-tuple-element.34), channel_id=1, source_target_pairs={{0,6},{1,7},{2,0},{3,1},{4,2},{5,3},{6,4},{7,5},{8,14},{9,15},{10,... | collective-permute-start | bytes 172040 | tf_op jit(solution)/shard_map/ppermute | solution.py:250
  497.8 19.1 %collective-permute-start.81 = (bf16[1,56,512]{2,0,1:T(2,128)(2,1)S(1)}, bf16[1,56,512]{2,0,1:T(2,128)(2,1)S(1)}, u32[]{:S(2)}, u32[]{:S(2)}) collective-permute-start(bf16[1,56,512]{2,0,1:T(2,128)(2,1)S(1)} %get-tuple-element.33), channel_id=1, source_target_pairs={{0,7},{1,0},{2,1},{3,2},{4,3},{5,4},{6,5},{7,6},{8,15},{9,8},{10,9... | collective-permute-start | bytes 172040 | tf_op jit(solution)/shard_map/ppermute | solution.py:250
  (30 other events, 475.6 us)
